TPU v7x, 256 devices: a whole 4x4x8 slice. The times are simulated.
256 devices in a mesh: lat: 128 (over x, z, y), lev: 2 (over core).
Axes of the slice: x: 4, y: 4, z: 8, core: 2. Of those that a mesh axis runs over, the one named last changes fastest.
Arguments:
- fields: float32 [1280, 3, 16, 2560], P('lat', None, 'lev'), may hold values from 0.1 to 5
- lat_fraction: float32 [1280], P('lat'), may hold values from 0 to 1
- lon_fraction: float32 [1280], P('lat'), may hold values from 0 to 1
- lon_shift: int32 [1280], P('lat'), may hold values from 0 to 2559
- departure_row: int32 [1280], P('lat'), may hold values from 1 to 1277, as said below
- extents: int32 [128, 2], P('lat'), may hold values from 1 to 4
Outputs:
- advected: float32 [1280, 3, 16, 2560], P('lat', None, 'lev')
Inputs may be any that keep to these rules, and one draw needn't show every extreme that they name: departure_row[r] lies within 39 rows of r.
All inputs are finite; a program needn't handle non-finite values.
Results may differ from a plain program's by a relative error of at most 0.0003.
Values sent between devices are 32-bit elements; how exact they have to be, the bound alone decides.
A program may use at most 128 MiB of HBM per device.

v0:
```python
import math

import jax
import jax.numpy as jnp
from jax import lax
from jax.sharding import Mesh
from jax.sharding import PartitionSpec as P

REACH = 4
LAT = ("lat_0", "lat_1", "lat_2")
LAT_LEV = ("lat_0", "lat_1", "lat_2", "lev")


def from_behind(block, axis, distance):
    devices = range(lax.axis_size(axis))
    route = [(i - distance, i) for i in devices if i - distance in devices]
    return lax.ppermute(block, axis, route)


def one_axis_at_a_time(array, axes):
    for axis in axes:
        array = lax.psum(array, axis)
    return array


def cubic_weights(fraction):
    return jnp.stack(
        [
            -fraction * (fraction - 1.0) * (fraction - 2.0) / 6.0,
            (fraction + 1.0) * (fraction - 1.0) * (fraction - 2.0) / 2.0,
            -(fraction + 1.0) * fraction * (fraction - 2.0) / 2.0,
            (fraction + 1.0) * fraction * (fraction - 1.0) / 6.0,
        ]
    )


def along_lon(column, lon_w, shift_value):
    lon_count = column.shape[-1]
    doubled = jnp.concatenate([column, column], axis=-1)
    result = jnp.zeros_like(column)
    for offset in range(4):
        first = (shift_value + offset - 1) % lon_count
        result = result + lon_w[offset] * lax.dynamic_slice_in_dim(doubled, first, lon_count, 2)
    return result


def per_device(fields, lat_fraction, lon_fraction, lon_shift, departure_row, extents):
    row_count = fields.shape[0]
    band_index = lax.axis_index(LAT)
    total_rows = lax.axis_size(LAT) * row_count
    first_row = band_index * row_count
    north_bands = []
    south_bands = []
    band_piece = fields
    for distance in range(REACH):
        band_piece = from_behind(band_piece, LAT, 1)
        north_bands.insert(0, band_piece)
    band_piece = fields
    for distance in range(REACH):
        band_piece = from_behind(band_piece, LAT, -1)
        south_bands.append(band_piece)
    padded = jnp.concatenate(north_bands + [fields] + south_bands, axis=0)
    low_bound = first_row - extents[0, 0] * row_count + 1
    high_bound = first_row + row_count - 3 + extents[0, 1] * row_count
    departure = jnp.clip(jnp.clip(departure_row, low_bound, high_bound), 1, total_rows - 3)
    local_start = departure - 1 - (first_row - REACH * row_count)

    def one_row(inputs):
        start_value, lat_t, lon_t, shift_value = inputs
        row_block = lax.dynamic_slice_in_dim(padded, start_value, 4, 0)
        lat_w = cubic_weights(lat_t)
        column = (
            lat_w[0] * row_block[0]
            + lat_w[1] * row_block[1]
            + lat_w[2] * row_block[2]
            + lat_w[3] * row_block[3]
        )
        return along_lon(column, cubic_weights(lon_t), shift_value)

    moved = lax.map(one_row, (local_start, lat_fraction, lon_fraction, lon_shift))
    row_ids = first_row + jnp.arange(row_count, dtype=jnp.int32)
    area = jnp.cos(math.pi * (row_ids.astype(jnp.float32) + 0.5) / total_rows - math.pi / 2.0)
    local_before = jnp.sum(area[:, None, None, None] * fields, axis=(0, 2, 3))
    local_after = jnp.sum(area[:, None, None, None] * moved, axis=(0, 2, 3))
    mass_before, mass_after = (
        one_axis_at_a_time(local_before, LAT_LEV),
        one_axis_at_a_time(local_after, LAT_LEV),
    )
    return moved * (mass_before / mass_after)[None, :, None, None]


def solution(mesh):
    finer = Mesh(
        mesh.devices.reshape(4, 8, 4, mesh.shape["lev"]), ("lat_0", "lat_1", "lat_2", "lev")
    )
    placed = (P(LAT, None, "lev", None), P(LAT), P(LAT), P(LAT), P(LAT), P(LAT, None))
    return jax.shard_map(
        per_device,
        mesh=finer,
        in_specs=placed,
        out_specs=P(LAT, None, "lev", None),
        check_vma=False,
    )
```

profile of v0, /device:TPU:8, one launch (start us, length us, event | category | flops | bytes accessed | tf_op | source)
XLA Modules:
  0.0 471.6 jit_solution(14239120991809122161)
XLA Ops:
  0.0 3.5 collective-permute-start
  3.5 2.5 collective-permute-start.4
  6.0 51.2 %collective-permute-done = f32[10,3,8,2560]{3,2,1,0:T(8,128)S(1)} collective-permute-done((f32[10,3,8,2560]{3,2,1,0:T(8,128)}, f32[10,3,8,2560]{3,2,1,0:T(8,128)S(1)}, u32[]{:S(2)}, u32[]{:S(2)}) %collective-permute-start) | collective-permute-done | bytes 2457632 | tf_op jit(solution)/shard_map/ppermute | solution.py:17
  57.2 3.5 collective-permute-start.1
  60.7 2.5 collective-permute-start.5
  63.2 50.1 %collective-permute-done.1 = f32[10,3,8,2560]{3,2,1,0:T(8,128)S(1)} collective-permute-done((f32[10,3,8,2560]{3,2,1,0:T(8,128)S(1)}, f32[10,3,8,2560]{3,2,1,0:T(8,128)S(1)}, u32[]{:S(2)}, u32[]{:S(2)}) %collective-permute-start.1) | collective-permute-done | bytes 2457632 | tf_op jit(solution)/shard_map/ppermute | solution.py:17
  113.3 3.5 collective-permute-start.2
  116.8 3.7 collective-permute-start.6
  120.6 48.2 %collective-permute-done.2 = f32[10,3,8,2560]{3,2,1,0:T(8,128)} collective-permute-done((f32[10,3,8,2560]{3,2,1,0:T(8,128)S(1)}, f32[10,3,8,2560]{3,2,1,0:T(8,128)}, u32[]{:S(2)}, u32[]{:S(2)}) %collective-permute-start.2) | collective-permute-done | bytes 2457632 | tf_op jit(solution)/shard_map/ppermute | solution.py:17
  168.8 3.5 collective-permute-start.3
  172.3 1.4 fusion.17
  175.1 0.7 add_subtract_fusion
  175.8 3.8 collective-permute-start.7
  179.6 44.1 %collective-permute-done.3 = f32[10,3,8,2560]{3,2,1,0:T(8,128)} collective-permute-done((f32[10,3,8,2560]{3,2,1,0:T(8,128)}, f32[10,3,8,2560]{3,2,1,0:T(8,128)}, u32[]{:S(2)}, u32[]{:S(2)}) %collective-permute-start.3) | collective-permute-done | bytes 2457632 | tf_op jit(solution)/shard_map/ppermute | solution.py:17
  223.6 1.9 constant_dynamic-update-slice_fusion.8
  225.5 2.0 constant_dynamic-update-slice_fusion.7
  228.1 1.5 copy-done.5
  229.8 1.5 copy-done
  231.5 1.5 copy-done.3
  233.2 1.9 constant_dynamic-update-slice_fusion.2
  235.1 1.9 constant_dynamic-update-slice_fusion.1
  237.2 7.3 %copy-done.1 = f32[90,3,8,2560]{3,2,1,0:T(8,128)} copy-done((f32[90,3,8,2560]{3,2,1,0:T(8,128)}, f32[90,3,8,2560]{3,2,1,0:T(8,128)S(1)}, u32[]{:S(2)}) %copy-start.1) | copy-done | bytes 22118424
  244.5 167.7 %while.15 = (s32[]{:T(128)}, f32[10,3,8,2560]{3,2,1,0:T(8,128)S(1)}, f32[10]{0:T(128)S(1)}, f32[10]{0:T(128)S(1)}, s32[10]{0:T(128)S(1)}, /*index=5*/f32[90,3,8,...) while((s32[]{:T(128)}, ...), condition=%wide.region_1.2_spmd, body=%wide.region_0.1_spmd.sunk | while | flops 1106001 | bytes 1721515 | solution.py:80
  249.0 0.6 dynamic_slice.169
  251.5 1.4 fusion.20
  252.9 0.6 dynamic_slice.168
  256.2 0.6 dynamic_slice.171
  260.7 0.6 fusion.21
  265.8 0.6 dynamic_slice.169
  268.3 1.4 fusion.20
  269.7 0.6 dynamic_slice.168
  277.4 0.6 fusion.21
  285.1 1.4 fusion.20
  294.2 0.6 fusion.21
  299.3 0.6 dynamic_slice.169
  301.8 1.4 fusion.20
  306.5 0.6 dynamic_slice.171
  311.0 0.6 fusion.21
  316.1 0.6 dynamic_slice.169
  318.6 1.4 fusion.20
  323.3 0.6 dynamic_slice.171
  327.7 0.6 fusion.21
  332.8 0.6 dynamic_slice.169
  335.4 1.4 fusion.20
  340.0 0.6 dynamic_slice.171
  344.5 0.6 fusion.21
  349.6 0.6 dynamic_slice.169
  352.1 1.4 fusion.20
  353.5 0.6 dynamic_slice.168
  361.3 0.6 fusion.21
  368.9 1.4 fusion.20
  370.3 0.6 dynamic_slice.168
  378.0 0.6 fusion.21
  385.7 1.4 fusion.20
  387.1 0.6 dynamic_slice.168
  394.8 0.6 fusion.21
  402.4 1.4 fusion.20
  411.6 0.6 fusion.21
  412.2 2.3 multiply_reduce_fusion
  414.5 25.1 %all-reduce.2 = (f32[3]{0:T(128)S(1)}, f32[3]{0:T(128)S(1)}) all-reduce(f32[3]{0:T(128)S(1)} %get-tuple-element.190, f32[3]{0:T(128)S(1)} %get-tuple-element.189), channel_id=1, replica_groups=mesh['lat_0'=4,'lat_1'=8,'lat_2'=4,'lev'=2] {'lat_0'}, use_global_device_ids=true, to_apply=%region_3.4 | all-reduce | flops 6 | bytes 48 | tf_op jit(solution)/shard_map/psum | solution.py:22
  439.6 14.1 %all-reduce = (f32[3]{0:T(128)S(1)}, f32[3]{0:T(128)S(1)}) all-reduce(f32[3]{0:T(128)S(1)} %get-tuple-element.209, f32[3]{0:T(128)S(1)} %get-tuple-element.210), channel_id=1, replica_groups=mesh['lat_0'=4,'lat_1'=8,'lat_2'=4,'lev'=2] {'lat_1'}, use_global_device_ids=true, to_apply=%region_4.5 | all-reduce | flops 6 | bytes 48 | tf_op jit(solution)/shard_map/psum | solution.py:22
  453.7 13.7 %all-reduce.1 = (f32[3]{0:T(128)S(1)}, f32[3]{0:T(128)S(1)}) all-reduce(f32[3]{0:T(128)S(1)} %get-tuple-element.205, f32[3]{0:T(128)S(1)} %get-tuple-element.206), channel_id=1, replica_groups=mesh['lat_0'=4,'lat_1'=8,'lat_2'=4,'lev'=2] {'lat_2'}, use_global_device_ids=true, to_apply=%region_5.6 | all-reduce | flops 6 | bytes 48 | tf_op jit(solution)/shard_map/psum | solution.py:22
  467.4 2.5 all-reduce.3
  469.9 1.8 broadcast_multiply_fusion
  (55 shorter events, 16.1 us)
Async XLA Ops:
  0.0 57.2 %collective-permute-start = (f32[10,3,8,2560]{3,2,1,0:T(8,128)}, f32[10,3,8,2560]{3,2,1,0:T(8,128)S(1)}, u32[]{:S(2)}, u32[]{:S(2)}) collective-permute-start(f32[10,3,8,2560]{3,2,1,0:T(8,128)} %param.8), channel_id=1, source_target_pairs={{0,2},{2,4},{4,6},{6,8},{8,10},{10,12},{12,14},{14,16},{16,18},{18... | collective-permute-start | bytes 7372808 | tf_op jit(solution)/shard_map/ppermute | solution.py:17
  3.5 57.2 %collective-permute-start.4 = (f32[10,3,8,2560]{3,2,1,0:T(8,128)}, f32[10,3,8,2560]{3,2,1,0:T(8,128)S(1)}, u32[]{:S(2)}, u32[]{:S(2)}) collective-permute-start(f32[10,3,8,2560]{3,2,1,0:T(8,128)} %param.8), channel_id=1, source_target_pairs={{2,0},{4,2},{6,4},{8,6},{10,8},{12,10},{14,12},{16,14},{18,16},{20... | collective-permute-start | bytes 7372808 | tf_op jit(solution)/shard_map/ppermute | solution.py:17
  57.2 115.1 %copy-start.4 = (f32[10,3,8,2560]{3,2,1,0:T(8,128)}, f32[10,3,8,2560]{3,2,1,0:T(8,128)S(1)}, u32[]{:S(2)}) copy-start(f32[10,3,8,2560]{3,2,1,0:T(8,128)S(1)} %collective-permute-done) | copy-start | bytes 7372804
  57.2 56.1 %collective-permute-start.1 = (f32[10,3,8,2560]{3,2,1,0:T(8,128)S(1)}, f32[10,3,8,2560]{3,2,1,0:T(8,128)S(1)}, u32[]{:S(2)}, u32[]{:S(2)}) collective-permute-start(f32[10,3,8,2560]{3,2,1,0:T(8,128)S(1)} %collective-permute-done), channel_id=1, source_target_pairs={{0,2},{2,4},{4,6},{6,8},{8,10},{10,12},{12,14},{14,16},{16,18},{18... | collective-permute-start | bytes 7372808 | tf_op jit(solution)/shard_map/ppermute | solution.py:17
  60.7 111.6 %copy-start.2 = (f32[10,3,8,2560]{3,2,1,0:T(8,128)}, f32[10,3,8,2560]{3,2,1,0:T(8,128)S(1)}, u32[]{:S(2)}) copy-start(f32[10,3,8,2560]{3,2,1,0:T(8,128)S(1)} %collective-permute-done.4) | copy-start | bytes 7372804
  60.7 56.1 %collective-permute-start.5 = (f32[10,3,8,2560]{3,2,1,0:T(8,128)S(1)}, f32[10,3,8,2560]{3,2,1,0:T(8,128)}, u32[]{:S(2)}, u32[]{:S(2)}) collective-permute-start(f32[10,3,8,2560]{3,2,1,0:T(8,128)S(1)} %collective-permute-done.4), channel_id=1, source_target_pairs={{2,0},{4,2},{6,4},{8,6},{10,8},{12,10},{14,12},{16,14},{18,16},{20... | collective-permute-start | bytes 7372808 | tf_op jit(solution)/shard_map/ppermute | solution.py:17
  113.3 59.0 %copy-start.6 = (f32[10,3,8,2560]{3,2,1,0:T(8,128)}, f32[10,3,8,2560]{3,2,1,0:T(8,128)S(1)}, u32[]{:S(2)}) copy-start(f32[10,3,8,2560]{3,2,1,0:T(8,128)S(1)} %collective-permute-done.1) | copy-start | bytes 7372804
  113.3 55.5 %collective-permute-start.2 = (f32[10,3,8,2560]{3,2,1,0:T(8,128)S(1)}, f32[10,3,8,2560]{3,2,1,0:T(8,128)}, u32[]{:S(2)}, u32[]{:S(2)}) collective-permute-start(f32[10,3,8,2560]{3,2,1,0:T(8,128)S(1)} %collective-permute-done.1), channel_id=1, source_target_pairs={{0,2},{2,4},{4,6},{6,8},{8,10},{10,12},{12,14},{14,16},{16,18},{18... | collective-permute-start | bytes 7372808 | tf_op jit(solution)/shard_map/ppermute | solution.py:17
  116.8 59.0 %collective-permute-start.6 = (f32[10,3,8,2560]{3,2,1,0:T(8,128)}, f32[10,3,8,2560]{3,2,1,0:T(8,128)}, u32[]{:S(2)}, u32[]{:S(2)}) collective-permute-start(f32[10,3,8,2560]{3,2,1,0:T(8,128)} %collective-permute-done.5), channel_id=1, source_target_pairs={{2,0},{4,2},{6,4},{8,6},{10,8},{12,10},{14,12},{16,14},{18,16},{20... | collective-permute-start | bytes 7372808 | tf_op jit(solution)/shard_map/ppermute | solution.py:17
  168.8 54.8 %collective-permute-start.3 = (f32[10,3,8,2560]{3,2,1,0:T(8,128)}, f32[10,3,8,2560]{3,2,1,0:T(8,128)}, u32[]{:S(2)}, u32[]{:S(2)}) collective-permute-start(f32[10,3,8,2560]{3,2,1,0:T(8,128)} %collective-permute-done.2), channel_id=1, source_target_pairs={{0,2},{2,4},{4,6},{6,8},{8,10},{10,12},{12,14},{14,16},{16,18},{18... | collective-permute-start | bytes 7372808 | tf_op jit(solution)/shard_map/ppermute | solution.py:17
  175.8 61.2 %collective-permute-start.7 = (f32[10,3,8,2560]{3,2,1,0:T(8,128)}, f32[10,3,8,2560]{3,2,1,0:T(8,128)S(1)}, u32[]{:S(2)}, u32[]{:S(2)}) collective-permute-start(f32[10,3,8,2560]{3,2,1,0:T(8,128)} %collective-permute-done.6), channel_id=1, source_target_pairs={{2,0},{4,2},{6,4},{8,6},{10,8},{12,10},{14,12},{16,14},{18,16},{20... | collective-permute-start | bytes 7372808 | tf_op jit(solution)/shard_map/ppermute | solution.py:17
  225.5 2.4 copy-start.7
  227.9 1.7 copy-start.5
  229.6 1.7 copy-start
  231.3 1.7 copy-start.3
  236.9 7.6 %copy-start.8 = (f32[10]{0:T(128)S(1)}, f32[10]{0:T(128)}, u32[]{:S(2)}) copy-start(f32[10]{0:T(128)} %param.10) | copy-start | bytes 124
  236.9 7.6 %copy-start.9 = (f32[10]{0:T(128)S(1)}, f32[10]{0:T(128)}, u32[]{:S(2)}) copy-start(f32[10]{0:T(128)} %param.9) | copy-start | bytes 124
  237.0 7.6 %copy-start.10 = (s32[10]{0:T(128)S(1)}, s32[10]{0:T(128)}, u32[]{:S(2)}) copy-start(s32[10]{0:T(128)} %param.11) | copy-start | bytes 124
  237.2 7.3 %copy-start.1 = (f32[90,3,8,2560]{3,2,1,0:T(8,128)}, f32[90,3,8,2560]{3,2,1,0:T(8,128)S(1)}, u32[]{:S(2)}) copy-start(f32[90,3,8,2560]{3,2,1,0:T(8,128)S(1)} %constant_dynamic-update-slice_fusion) | copy-start | bytes 66355204
where the time goes:
time: 475 us; the launch traced here: 472 us
  waiting for transfers between devices  194 us (41%)
  loops' own time  124 us (26%)
  blocking collectives  55.3 us (12%)
  local copies, waits for them, and re-layouts  45.7 us (10%)
  starting transfers between devices  26.4 us (6%)
  other arithmetic  24.8 us (5%)
    ppermute x8, waiting for transfers between devices, from_behind(): return lax.ppermute(block, axis, route)  194 us
    another operation x1, loops' own time, per_device(): lax.map(one_row, (local_start, lat_fraction, lon_fraction, lon_shift))  124 us
    psum x4, blocking collectives, one_axis_at_a_time(): array = lax.psum(array, axis)  55.3 us
    ppermute x8, starting transfers between devices, from_behind(): return lax.ppermute(block, axis, route)  26.4 us
    dynamic_slice x40, local copies, waits for them, and re-layouts, per_device(): lax.map(one_row, (local_start, lat_fraction, lon_fraction, lon_shift))  23.5 us
    unnamed x30, local copies, waits for them, and re-layouts  20.6 us
    add x10, other arithmetic, one_row(): lat_w[0] * row_block[0] + lat_w[1] * row_block[1] + lat_w[2] * row_block[2]  13.8 us
  transfers between devices with their start and end apart: 8, of which 4 were waited for; matrix products, arithmetic and copies ran while one was open for 2% of the time, Pallas kernels for 0%

commit v1 on v0

v1 whole, which is shorter than its diff:
```python
import functools
import math

import jax
import jax.numpy as jnp
from jax import lax
from jax.experimental import pallas as pl
from jax.experimental.pallas import tpu as pltpu
from jax.sharding import Mesh
from jax.sharding import PartitionSpec as P

MESH = pl.DeviceIdType.MESH
LAT = ("x", "z", "y")
NX, NZ, NY = 4, 8, 4
LANES = 128
CHUNKS = [(f, a, b) for f in range(3) for a, b in ((0, 3), (3, 5))]


def cubic_weights(t):
    return (
        -t * (t - 1.0) * (t - 2.0) / 6.0,
        (t + 1.0) * (t - 1.0) * (t - 2.0) / 2.0,
        -(t + 1.0) * t * (t - 2.0) / 2.0,
        (t + 1.0) * t * (t - 1.0) / 6.0,
    )


def exchange_kernel(
    chunks, quarter, total_rows,
    fields, lat_fraction, lon_fraction, departure_row, extents,
    col_out, scale_out,
    *scratch,
):
    n = len(chunks)
    bufs, cols = scratch[:n], scratch[n : 2 * n]
    (own, meta_i, meta_f, smem_i, smem_f, weights, table, sums, sums_in,
     own_sem, piece_sem, yin_send, yin_recv, z_send, z_recv, mi_send, mi_recv, mf_send, mf_recv,
     smem_sem, tab_send, tab_recv, ar_send, ar_recv, out_send, out_recv, out_own) = scratch[2 * n :]
    rows = own.shape[0]
    group = NY * rows
    x, z, y = lax.axis_index("x"), lax.axis_index("z"), lax.axis_index("y")
    lev = lax.axis_index("lev")

    def y_peer(d):
        return {"y": lax.rem(y + d, NY)}

    def z_peer(direction):
        flat = lax.rem(x * NZ + z + direction + NX * NZ, NX * NZ)
        return {"x": flat // NZ, "z": lax.rem(flat, NZ)}

    def flipped(value, bit):
        return value + bit - 2 * bit * lax.rem(value // bit, 2)

    sum_peers = [
        {"lev": 1 - lev},
        {"z": flipped(z, 1)}, {"z": flipped(z, 2)}, {"z": flipped(z, 4)},
        {"x": flipped(x, 1)}, {"x": flipped(x, 2)},
    ]
    z_dirs = (1, -1)

    def lanes_of(c, which):
        first = which * quarter + chunks[c][1] * LANES
        return pl.ds(pl.multiple_of(first, LANES), (chunks[c][2] - chunks[c][1]) * LANES)

    def in_fields(c, which):
        return fields.at[:, chunks[c][0], :, lanes_of(c, which)]

    def group_rows(c, zone, which):
        return bufs[c].at[pl.ds(zone * group + which * rows, rows)]

    def yin(c, d):
        return pltpu.make_async_remote_copy(
            src_ref=in_fields(c, lax.rem(y + d, NY)), dst_ref=group_rows(c, 1, y),
            send_sem=yin_send.at[c, d - 1], recv_sem=yin_recv.at[c, d - 1],
            device_id=y_peer(d), device_id_type=MESH)

    def zmove(c, k, d):
        source = lax.rem(y - d + NY, NY)
        return pltpu.make_async_remote_copy(
            src_ref=in_fields(c, y) if d == 0 else group_rows(c, 1, source),
            dst_ref=group_rows(c, 0 if k == 0 else 2, source),
            send_sem=z_send.at[c, k, d], recv_sem=z_recv.at[c, k, d],
            device_id=z_peer(z_dirs[k]), device_id_type=MESH)

    def piece(c):
        return pltpu.make_async_copy(in_fields(c, y), group_rows(c, 1, y), piece_sem.at[c])

    def out_ref(c):
        return col_out.at[:, chunks[c][0], :, lanes_of(c, y)]

    def yout(c, d):
        return pltpu.make_async_remote_copy(
            src_ref=cols[c].at[pl.ds(lax.rem(y + d, NY) * rows, rows)], dst_ref=out_ref(c),
            send_sem=out_send.at[c, d - 1], recv_sem=out_recv.at[c, d - 1],
            device_id=y_peer(d), device_id_type=MESH)

    def yout_own(c):
        return pltpu.make_async_copy(cols[c].at[pl.ds(y * rows, rows)], out_ref(c), out_own.at[c])

    def meta(which, d):
        ref, s, r = ((meta_i, mi_send, mi_recv), (meta_f, mf_send, mf_recv))[which]
        return pltpu.make_async_remote_copy(
            src_ref=ref.at[y], dst_ref=ref.at[y], send_sem=s.at[d - 1], recv_sem=r.at[d - 1],
            device_id=y_peer(d), device_id_type=MESH)

    def table_move(k):
        return pltpu.make_async_remote_copy(
            src_ref=table.at[1], dst_ref=table.at[0 if k == 0 else 2], send_sem=tab_send.at[k], recv_sem=tab_recv.at[k],
            device_id=z_peer(z_dirs[k]), device_id_type=MESH)

    def sum_move(k):
        return pltpu.make_async_remote_copy(
            src_ref=sums.at[k], dst_ref=sums_in.at[k], send_sem=ar_send.at[k], recv_sem=ar_recv.at[k],
            device_id=sum_peers[k], device_id_type=MESH)

    barrier = pltpu.get_barrier_semaphore()
    partners = [y_peer(d) for d in (1, 2, 3)] + [z_peer(k) for k in z_dirs] + sum_peers
    for partner in partners:
        pl.semaphore_signal(barrier, inc=1, device_id=partner, device_id_type=MESH)
    own_copy = pltpu.make_async_copy(fields, own, own_sem)
    own_copy.start()
    for c in range(n):
        piece(c).start()

    lane = lax.broadcasted_iota(jnp.int32, (8, LANES), 1)
    sub = lax.broadcasted_iota(jnp.int32, (8, LANES), 0)
    first_group_row = (x * NZ + z) * group
    first_row = first_group_row + y * rows
    low = first_row - extents[0, 0] * rows + 1
    high = first_row + rows - 3 + extents[0, 1] * rows
    starts = jnp.zeros((8, LANES), jnp.int32)
    lat_t = jnp.zeros((8, LANES), jnp.float32)
    lon_t = jnp.zeros((8, LANES), jnp.float32)
    for p in range(rows):
        departure = jnp.minimum(jnp.maximum(departure_row[p], low), high)
        departure = jnp.minimum(jnp.maximum(departure, 1), total_rows - 3)
        here = lane == y * rows + p
        starts = jnp.where(here, departure - 1 - (first_group_row - group), starts)
        lat_t = jnp.where(here, lat_fraction[p], lat_t)
        lon_t = jnp.where(here, lon_fraction[p], lon_t)
    meta_i[y] = starts

    def area_at(row_ids):
        return jnp.cos(math.pi * (row_ids.astype(jnp.float32) + 0.5) / total_rows - math.pi / 2.0)

    lw = cubic_weights(lon_t)
    area_lon = area_at(first_group_row + lane) * (lw[0] + lw[1] + lw[2] + lw[3])
    mine = (lane >= y * rows) & (lane < (y + 1) * rows)
    facts = jnp.where(mine & (sub == 3), lat_t, jnp.where(mine & (sub == 7), area_lon, 0.0))

    pl.semaphore_wait(barrier, len(partners))

    def start_yin(c):
        for d in (2, 1, 3):
            yin(c, d).start()

    def start_zown(c):
        for k in range(2):
            zmove(c, k, 0).start()

    start_yin(0)
    start_zown(0)
    start_yin(1)
    start_zown(1)
    start_zown(2)

    own_copy.wait()

    def row_sums(p, facts):
        for f in range(3):
            row = own[p, f]
            vec = row[:, :LANES]
            for i in range(1, row.shape[1] // LANES):
                vec = vec + row[:, i * LANES : (i + 1) * LANES]
            value = jnp.sum(jnp.sum(vec, axis=1, keepdims=True), axis=0, keepdims=True)
            facts = jnp.where((lane == y * rows + p) & ((sub == f) | (sub == f + 4)), value, facts)
        return facts

    meta_f[y] = lax.fori_loop(0, rows, row_sums, facts)
    start_yin(2)
    for d in (1, 2, 3):
        meta(0, d).start()
        meta(1, d).start()

    def forward(c):
        for d in (1, 3, 2):
            yin(c, d).wait_recv()
            for k in range(2):
                zmove(c, k, d).start()

    forward(0)

    for d in (1, 2, 3):
        meta(0, d).wait_recv()
        meta(1, d).wait_recv()
    table[1] = meta_f[0] + meta_f[1] + meta_f[2] + meta_f[3]
    group_starts = meta_i[0] + meta_i[1] + meta_i[2] + meta_i[3]
    meta_i[NY] = group_starts
    forward(1)
    to_smem = [pltpu.make_async_copy(meta_i.at[NY], smem_i, smem_sem.at[0]),
               pltpu.make_async_copy(table.at[1], smem_f, smem_sem.at[1])]
    for copy in to_smem:
        copy.start()
    for k in range(2):
        table_move(k).start()
    for copy in to_smem:
        copy.wait()

    def row_weights(t, coefficient):
        start = smem_i[0, t]
        w = cubic_weights(jnp.full((8, LANES), smem_f[3, t], jnp.float32))
        area_t = smem_f[7, t]
        for a in range(4):
            weights[t, a] = w[a]
            coefficient = coefficient + jnp.where(lane == start + a, area_t * w[a], 0.0)
        return coefficient

    coefficient = lax.fori_loop(0, group, row_weights, jnp.zeros((8, LANES), jnp.float32))

    for c in range(n):
        if 3 <= c + 2 < n:
            start_yin(c + 2)
            start_zown(c + 2)
        if 2 <= c + 1 < n:
            forward(c + 1)
        if c == 0:
            for k in range(2):
                table_move(k).wait_recv()
            valid = (sub != 3) & (sub != 7) & (lane < group)
            parts = [jnp.where(valid, table[g], 0.0) for g in range(3)]
            whole = parts[0] + pltpu.roll(parts[1], group, 1) + pltpu.roll(parts[2], 2 * group, 1)
            in_group = (lane >= group) & (lane < 2 * group)
            area = jnp.where(in_group, area_at(first_group_row - group + lane), 0.0)
            sums[0] = whole * jnp.where(sub < 4, area, coefficient)
        else:
            sum_move(c - 1).wait_recv()
            sums[c] = sums[c - 1] + sums_in[c - 1]

        piece(c).wait()
        for k in range(2):
            for d in range(4):
                zmove(c, k, d).wait_recv()

        def column(i, carry, c=c):
            t = lax.rem(i + (y + 1) * rows, group)
            taps = bufs[c][pl.ds(smem_i[0, t], 4)]
            width = taps.shape[2] // LANES
            for j in range(width):
                s = slice(j * LANES, (j + 1) * LANES)
                cols[c][t, :, s] = (
                    weights[t, 0] * taps[0, :, s] + weights[t, 1] * taps[1, :, s]
                    + weights[t, 2] * taps[2, :, s] + weights[t, 3] * taps[3, :, s])
            return carry

        lax.fori_loop(0, group, column, 0)
        for d in (2, 1, 3):
            yout(c, d).start()
        sum_move(c).start()
        if c > 0:
            yout_own(c - 1).start()

    sum_move(n - 1).wait_recv()
    final = sums[n - 1] + sums_in[n - 1]
    yout_own(n - 1).start()
    mass = jnp.sum(final, axis=1, keepdims=True)
    for f in range(3):
        scale_out[f : f + 1, :] = jnp.broadcast_to(mass[f : f + 1] / mass[f + 4 : f + 5], (1, LANES))
    scale_out[3:8, :] = jnp.zeros((5, LANES), jnp.float32)
    for c in range(n):
        yout_own(c).wait()
        for d in (1, 2, 3):
            yout(c, d).wait_recv()
    for c in range(n):
        for d in (1, 2, 3):
            yin(c, d).wait_send()
            yout(c, d).wait_send()
        for k in range(2):
            for d in range(4):
                zmove(c, k, d).wait_send()
        sum_move(c).wait_send()
    for d in (1, 2, 3):
        meta(0, d).wait_send()
        meta(1, d).wait_send()
    for k in range(2):
        table_move(k).wait_send()


def lon_kernel(shift, fraction, scale, column, out, doubled):
    r = pl.program_id(0)
    lon = column.shape[-1]
    tiles = lon // LANES
    t = jnp.full((8, LANES), fraction[r], jnp.float32)
    w = [v[:1, :1] for v in cubic_weights(t)]
    base = lax.rem(shift[r] - 1 + lon, lon)
    whole = base // LANES
    part = base - whole * LANES
    turn = lax.rem(LANES - part, LANES)
    lane = lax.broadcasted_iota(jnp.int32, (8, LANES), 1)
    for f in range(3):
        data = column[0, f]
        doubled[:, :lon] = data
        doubled[:, lon:] = data
        row = doubled[:, pl.ds(pl.multiple_of(whole * LANES, LANES), lon)]
        mixed = row * w[0]
        for k in range(1, 4):
            row = pltpu.roll(row, lon - 1, 1)
            mixed = mixed + row * w[k]
        mixed = mixed * scale[f : f + 1, :1]
        turned = [pltpu.roll(mixed[:, i * LANES : (i + 1) * LANES], turn, 1) for i in range(tiles)]
        for i in range(tiles):
            out[0, f, :, i * LANES : (i + 1) * LANES] = jnp.where(
                lane < LANES - part, turned[i], turned[(i + 1) % tiles])


def per_device(fields, lat_fraction, lon_fraction, lon_shift, departure_row, extents):
    rows, n_fields, levels, lon = fields.shape
    quarter = lon // NY
    n = len(CHUNKS)
    group = NY * rows
    total_rows = NX * NZ * group
    f32, dma = jnp.float32, pltpu.SemaphoreType.DMA
    smem = pl.BlockSpec(memory_space=pltpu.SMEM)
    widths = [(b - a) * LANES for _, a, b in CHUNKS]
    column, scale = pl.pallas_call(
        functools.partial(exchange_kernel, CHUNKS, quarter, total_rows),
        out_shape=(jax.ShapeDtypeStruct(fields.shape, f32), jax.ShapeDtypeStruct((8, LANES), f32)),
        in_specs=[pl.BlockSpec(memory_space=pl.ANY)] + [smem] * 4,
        out_specs=(pl.BlockSpec(memory_space=pl.ANY), pl.BlockSpec(memory_space=pltpu.VMEM)),
        scratch_shapes=[pltpu.VMEM((3 * group, levels, w), f32) for w in widths]
        + [pltpu.VMEM((group, levels, w), f32) for w in widths]
        + [
            pltpu.VMEM(fields.shape, f32),
            pltpu.VMEM((NY + 1, 8, LANES), jnp.int32),
            pltpu.VMEM((NY, 8, LANES), f32),
            pltpu.SMEM((8, LANES), jnp.int32),
            pltpu.SMEM((8, LANES), f32),
            pltpu.VMEM((group, 4, 8, LANES), f32),
            pltpu.VMEM((3, 8, LANES), f32),
            pltpu.VMEM((6, 8, LANES), f32),
            pltpu.VMEM((6, 8, LANES), f32),
            dma(()), dma((n,)), dma((n, 3)), dma((n, 3)), dma((n, 2, 4)), dma((n, 2, 4)),
            dma((3,)), dma((3,)), dma((3,)), dma((3,)), dma((2,)), dma((2,)), dma((2,)), dma((6,)), dma((6,)),
            dma((n, 3)), dma((n, 3)), dma((n,)),
        ],
        compiler_params=pltpu.CompilerParams(collective_id=0, has_side_effects=True, vmem_limit_bytes=40 << 20),
    )(fields, lat_fraction, lon_fraction, departure_row, extents)
    return pl.pallas_call(
        lon_kernel,
        grid=(rows,),
        out_shape=jax.ShapeDtypeStruct(fields.shape, f32),
        in_specs=[smem, smem, pl.BlockSpec((8, LANES), lambda r: (0, 0)),
                  pl.BlockSpec((1, n_fields, levels, lon), lambda r: (r, 0, 0, 0))],
        out_specs=pl.BlockSpec((1, n_fields, levels, lon), lambda r: (r, 0, 0, 0)),
        scratch_shapes=[pltpu.VMEM((levels, 2 * lon), f32)],
    )(lon_shift, lon_fraction, scale, column)


def solution(mesh):
    finer = Mesh(mesh.devices.reshape(NX, NZ, NY, mesh.shape["lev"]), LAT + ("lev",))
    placed = (P(LAT, None, "lev", None), P(LAT), P(LAT), P(LAT), P(LAT), P(LAT, None))
    return jax.shard_map(
        per_device, mesh=finer, in_specs=placed, out_specs=P(LAT, None, "lev", None), check_vma=False)
```

time: 475 us -> 94.1 us (0.20)
  waiting for transfers between devices: 194 us -> 0 us
  loops' own time: 124 us -> 0 us
  Pallas kernels: 0 us -> 87.4 us
  blocking collectives: 55.3 us -> 0 us
  local copies, waits for them, and re-layouts: 45.7 us -> 6.33 us
  starting transfers between devices: 26.4 us -> 0 us
  other arithmetic: 24.8 us -> 0 us
    ppermute x8 -> x0, waiting for transfers between devices: 194 us -> none  [from_behind(): return lax.ppermute(block, axis, route)]
    another operation x1 -> x0, loops' own time: 124 us -> none  [per_device(): lax.map(one_row, (local_start, lat_fraction, lon_fraction, lon_shift))]
    pallas_call x0 -> x2, Pallas kernels: none -> 87.4 us  [the longest x1 79 us: per_device(): pl.pallas_call(functools.partial(exchange_kernel, CHUNKS, quarter, total_...]
    psum x4 -> x0, blocking collectives: 55.3 us -> none  [one_axis_at_a_time(): array = lax.psum(array, axis)]
    ppermute x8 -> x0, starting transfers between devices: 26.4 us -> none  [from_behind(): return lax.ppermute(block, axis, route)]
    dynamic_slice x40 -> x0, local copies, waits for them, and re-layouts: 23.5 us -> none  [per_device(): lax.map(one_row, (local_start, lat_fraction, lon_fraction, lon_shift))]
    unnamed x30 -> x14, local copies, waits for them, and re-layouts: 20.6 us -> 6.33 us
    add x10 -> x0, other arithmetic: 13.8 us -> none  [one_row(): lat_w[0] * row_block[0] + lat_w[1] * row_block[1] + lat_w[2] * row_block[2]]
  transfers between devices with their start and end apart: 8 -> 0, of which waited for: 4 -> 0; matrix products, arithmetic and copies ran while one was open for 2% -> 0% of each run, Pallas kernels for 0% -> 0%
where the time goes in v1:
time: 94.1 us; the launch traced here: 93.8 us
  Pallas kernels  87.4 us (93%)
  local copies, waits for them, and re-layouts  6.33 us (7%)
    pallas_call x1, Pallas kernels, per_device(): pl.pallas_call(functools.partial(exchange_kernel, CHUNKS, quarter, total_...  79 us
    pallas_call x1, Pallas kernels, per_device(): pl.pallas_call(lon_kernel, grid=(rows,), out_shape=jax.ShapeDtypeStruct(f...  8.44 us
    unnamed x14, local copies, waits for them, and re-layouts  6.33 us

profile of v1, /device:TPU:8, one launch (start us, length us, event | category | flops | bytes accessed | tf_op | source)
XLA Modules:
  0.0 93.8 jit_solution(4792316155200813901)
XLA Ops:
  0.0 0.0 copy-start
  0.0 1.7 %copy-done = f32[10,3,8,2560]{3,2,1,0:T(8,128)S(1)} copy-done((f32[10,3,8,2560]{3,2,1,0:T(8,128)S(1)}, f32[10,3,8,2560]{3,2,1,0:T(8,128)}, u32[]{:S(2)}) %copy-start) | copy-done | bytes 2457624
  1.7 0.0 copy-start.3
  1.7 0.7 copy-done.3
  2.4 0.0 copy-start.4
  2.4 0.7 copy-done.4
  3.0 0.0 copy-start.5
  3.0 0.7 copy-done.5
  3.7 0.0 copy-start.6
  3.7 0.7 copy-done.6
  4.3 79.0 %shard_map.64 = (f32[10,3,8,2560]{3,2,1,0:T(8,128)S(1)}, f32[8,128]{1,0:T(8,128)S(1)}) custom-call(f32[10,3,8,2560]{3,2,1,0:T(8,128)S(1)} %copy-done, f32[10]{0:T(128)S(1)} %copy-done.4, f32[10]{0:T(128)S(1)} %copy-done.3, s32[10]{0:T(128)S(1)} %copy-done.5, s32[1,2]{1,0:T(1,128)S(1)} %copy-done.6), custom_call_target="tpu_custom_call" | custom-call | tf_op jit(solution)/shard_map/pallas_call | solution.py:324
  83.3 0.0 copy-start.1
  83.3 1.4 %copy-done.1 = f32[10,3,8,2560]{3,2,1,0:T(8,128)} copy-done((f32[10,3,8,2560]{3,2,1,0:T(8,128)}, f32[10,3,8,2560]{3,2,1,0:T(8,128)S(1)}, u32[]{:S(2)}) %copy-start.1) | copy-done | bytes 2457624
  84.8 0.0 copy-start.2
  84.8 0.6 copy-done.2
  85.3 8.4 %shard_map.65 = f32[10,3,8,2560]{3,2,1,0:T(8,128)} custom-call(s32[10]{0:T(128)} %shift.1, f32[10]{0:T(128)} %fraction.1, f32[8,128]{1,0:T(8,128)} %copy-done.2, f32[10,3,8,2560]{3,2,1,0:T(8,128)} %copy-done.1), custom_call_target="tpu_custom_call" | custom-call | tf_op jit(solution)/shard_map/pallas_call | solution.py:347
Async XLA Ops:
  0.0 1.7 %copy-start = (f32[10,3,8,2560]{3,2,1,0:T(8,128)S(1)}, f32[10,3,8,2560]{3,2,1,0:T(8,128)}, u32[]{:S(2)}) copy-start(f32[10,3,8,2560]{3,2,1,0:T(8,128)} %fields.1) | copy-start | bytes 7372804
  1.7 0.7 copy-start.3
  2.4 0.7 copy-start.4
  3.0 0.7 copy-start.5
  3.7 0.7 copy-start.6
  83.3 1.4 %copy-start.1 = (f32[10,3,8,2560]{3,2,1,0:T(8,128)}, f32[10,3,8,2560]{3,2,1,0:T(8,128)S(1)}, u32[]{:S(2)}) copy-start(f32[10,3,8,2560]{3,2,1,0:T(8,128)S(1)} %get-tuple-element.8.column) | copy-start | bytes 7372804
  84.8 0.6 copy-start.2

commit v2 on v1

v2 whole, which is shorter than its diff:
```python
import functools
import math

import jax
import jax.numpy as jnp
from jax import lax
from jax.experimental import pallas as pl
from jax.experimental.pallas import tpu as pltpu
from jax.sharding import Mesh
from jax.sharding import PartitionSpec as P

MESH = pl.DeviceIdType.MESH
LAT = ("x", "z", "y")
NX, NZ, NY = 4, 8, 4
LANES = 128
CHUNKS = [(0, 0, 3), (0, 3, 5), (1, 0, 3), (1, 3, 5), (2, 0, 2), (2, 2, 4), (2, 4, 5)]
LON_TURN = {5: (0, 1)}
X_SUM_TURN = 3
AHEAD = 2


def cubic_weights(t):
    return (
        -t * (t - 1.0) * (t - 2.0) / 6.0,
        (t + 1.0) * (t - 1.0) * (t - 2.0) / 2.0,
        -(t + 1.0) * t * (t - 2.0) / 2.0,
        (t + 1.0) * t * (t - 1.0) / 6.0,
    )


def split(value):
    scaled = value * 65537.0
    high = scaled - (scaled - value)
    return high.astype(jnp.bfloat16), (value - high).astype(jnp.bfloat16)


def exchange_kernel(
    chunks, quarter, total_rows,
    fields, lat_fraction_in, lon_fraction_in, lon_shift_in, departure_row_in, extents_in,
    moved,
    *scratch,
):
    n = len(chunks)
    lon = NY * quarter
    bufs, cols, full, doubled = scratch[:n], scratch[n : 2 * n], scratch[2 * n : 2 * n + 3], scratch[2 * n + 3 : 2 * n + 5]
    (lat_fraction, lon_fraction, lon_shift, departure_row, extents, small_sem, lon_weights, scales,
     own, meta_i, meta_f, smem_i, smem_f, weights, table, sums, sums_in,
     own_sem, piece_sem, yin_send, yin_recv, z_send, z_recv, mi_send, mi_recv, mf_send, mf_recv,
     smem_sem, tab_send, tab_recv, ar_send, ar_recv, out_send, out_recv) = scratch[2 * n + 5 :]
    rows = own.shape[0]
    group = NY * rows
    x, z, y = lax.axis_index("x"), lax.axis_index("z"), lax.axis_index("y")
    lev = lax.axis_index("lev")

    def y_peer(d):
        return {"y": lax.rem(y + d, NY)}

    def z_peer(direction):
        flat = lax.rem(x * NZ + z + direction + NX * NZ, NX * NZ)
        return {"x": flat // NZ, "z": lax.rem(flat, NZ)}

    sum_peers = [
        [{"lev": 1 - lev}],
        [{"x": lax.rem(x + d, NX)} for d in range(1, NX)],
        [{"z": lax.rem(z + d, NZ)} for d in range(1, NZ)],
    ]
    z_dirs = (1, -1)

    def lanes_of(c, which):
        first = which * quarter + chunks[c][1] * LANES
        return pl.ds(pl.multiple_of(first, LANES), (chunks[c][2] - chunks[c][1]) * LANES)

    def in_fields(c, which):
        return fields.at[:, chunks[c][0], :, lanes_of(c, which)]

    def group_rows(c, zone, which):
        return bufs[c].at[pl.ds(zone * group + which * rows, rows)]

    def yin(c, d):
        return pltpu.make_async_remote_copy(
            src_ref=in_fields(c, lax.rem(y + d, NY)), dst_ref=group_rows(c, 1, y),
            send_sem=yin_send.at[c, d - 1], recv_sem=yin_recv.at[c, d - 1],
            device_id=y_peer(d), device_id_type=MESH)

    def zmove(c, k, d):
        source = lax.rem(y - d + NY, NY)
        return pltpu.make_async_remote_copy(
            src_ref=in_fields(c, y) if d == 0 else group_rows(c, 1, source),
            dst_ref=group_rows(c, 0 if k == 0 else 2, source),
            send_sem=z_send.at[c, k, d], recv_sem=z_recv.at[c, k, d],
            device_id=z_peer(z_dirs[k]), device_id_type=MESH)

    def piece(c):
        return pltpu.make_async_copy(in_fields(c, y), group_rows(c, 1, y), piece_sem.at[c])

    def out_ref(c):
        return full[chunks[c][0]].at[:, :, lanes_of(c, y)]

    def yout(c, d):
        return pltpu.make_async_remote_copy(
            src_ref=cols[c].at[pl.ds(lax.rem(y + d, NY) * rows, rows)], dst_ref=out_ref(c),
            send_sem=out_send.at[c, d - 1], recv_sem=out_recv.at[c, d - 1],
            device_id=y_peer(d), device_id_type=MESH)

    def meta(which, d):
        ref, s, r = ((meta_i, mi_send, mi_recv), (meta_f, mf_send, mf_recv))[which]
        return pltpu.make_async_remote_copy(
            src_ref=ref.at[y], dst_ref=ref.at[y], send_sem=s.at[d - 1], recv_sem=r.at[d - 1],
            device_id=y_peer(d), device_id_type=MESH)

    def table_move(k):
        return pltpu.make_async_remote_copy(
            src_ref=table.at[1], dst_ref=table.at[0 if k == 0 else 2], send_sem=tab_send.at[k], recv_sem=tab_recv.at[k],
            device_id=z_peer(z_dirs[k]), device_id_type=MESH)

    def sum_moves(step):
        first = sum(len(peers) for peers in sum_peers[:step])
        return [
            pltpu.make_async_remote_copy(
                src_ref=sums.at[step], dst_ref=sums_in.at[first + i],
                send_sem=ar_send.at[first + i], recv_sem=ar_recv.at[first + i],
                device_id=peer, device_id_type=MESH)
            for i, peer in enumerate(sum_peers[step])
        ]

    barrier = pltpu.get_barrier_semaphore()
    partners = [y_peer(d) for d in (1, 2, 3)] + [z_peer(k) for k in z_dirs] + sum(sum_peers, [])
    for partner in partners:
        pl.semaphore_signal(barrier, inc=1, device_id=partner, device_id_type=MESH)
    small = [
        pltpu.make_async_copy(src, dst, small_sem.at[i])
        for i, (src, dst) in enumerate((
            (departure_row_in, departure_row), (extents_in, extents), (lat_fraction_in, lat_fraction),
            (lon_fraction_in, lon_fraction), (lon_shift_in, lon_shift)))
    ]
    for copy in small:
        copy.start()
    own_copy = pltpu.make_async_copy(fields, own, own_sem)
    own_copy.start()
    for c in range(n):
        piece(c).start()

    for copy in small:
        copy.wait()

    lane = lax.broadcasted_iota(jnp.int32, (8, LANES), 1)
    sub = lax.broadcasted_iota(jnp.int32, (8, LANES), 0)
    first_group_row = (x * NZ + z) * group
    first_row = first_group_row + y * rows
    low = first_row - extents[0, 0] * rows + 1
    high = first_row + rows - 3 + extents[0, 1] * rows
    starts = jnp.zeros((8, LANES), jnp.int32)
    lat_t = jnp.zeros((8, LANES), jnp.float32)
    lon_t = jnp.zeros((8, LANES), jnp.float32)
    for p in range(rows):
        departure = jnp.minimum(jnp.maximum(departure_row[p], low), high)
        departure = jnp.minimum(jnp.maximum(departure, 1), total_rows - 3)
        here = lane == y * rows + p
        starts = jnp.where(here, departure - 1 - (first_group_row - group), starts)
        lat_t = jnp.where(here, lat_fraction[p], lat_t)
        lon_t = jnp.where(here, lon_fraction[p], lon_t)
    meta_i[y] = starts

    def area_at(row_ids):
        return jnp.cos(math.pi * (row_ids.astype(jnp.float32) + 0.5) / total_rows - math.pi / 2.0)

    lw = cubic_weights(lon_t)
    area_lon = area_at(first_group_row + lane) * (lw[0] + lw[1] + lw[2] + lw[3])
    mine = (lane >= y * rows) & (lane < (y + 1) * rows)
    facts = jnp.where(mine & (sub == 3), lat_t, jnp.where(mine & (sub == 7), area_lon, 0.0))

    own_copy.wait()

    def row_sums(p, facts):
        for f in range(3):
            row = own[p, f]
            vec = row[:, :LANES]
            for i in range(1, row.shape[1] // LANES):
                vec = vec + row[:, i * LANES : (i + 1) * LANES]
            value = jnp.sum(jnp.sum(vec, axis=1, keepdims=True), axis=0, keepdims=True)
            facts = jnp.where((lane == y * rows + p) & ((sub == f) | (sub == f + 4)), value, facts)
        return facts

    meta_f[y] = lax.fori_loop(0, rows, row_sums, facts)
    pl.semaphore_wait(barrier, len(partners))
    for d in (1, 2, 3):
        meta(0, d).start()
        meta(1, d).start()

    def start_yin(c):
        for d in (2, 1, 3):
            yin(c, d).start()

    def start_zown(c):
        for k in range(2):
            zmove(c, k, 0).start()

    def forward(c):
        for d in (1, 3, 2):
            yin(c, d).wait_recv()
            for k in range(2):
                zmove(c, k, d).start()

    for c in range(n):
        if c < AHEAD:
            start_zown(c)
        start_yin(c)

    for d in (1, 2, 3):
        meta(0, d).wait_recv()
        meta(1, d).wait_recv()
    table[1] = meta_f[0] + meta_f[1] + meta_f[2] + meta_f[3]
    group_starts = meta_i[0] + meta_i[1] + meta_i[2] + meta_i[3]
    meta_i[NY] = group_starts
    to_smem = [pltpu.make_async_copy(meta_i.at[NY], smem_i, smem_sem.at[0]),
               pltpu.make_async_copy(table.at[1], smem_f, smem_sem.at[1])]
    for copy in to_smem:
        copy.start()
    for k in range(2):
        table_move(k).start()
    def row_weights(t, coefficient):
        start = smem_i[0, t]
        w = cubic_weights(jnp.full((8, LANES), smem_f[3, t], jnp.float32))
        area_t = smem_f[7, t]
        for a in range(4):
            weights[t, a] = w[a]
            coefficient = coefficient + jnp.where(lane == start + a, area_t * w[a], 0.0)
        return coefficient

    def longitude_matrix(p, carry):
        part = lax.rem(lon_shift[p] - 1 + lon, LANES)
        ahead = (lax.broadcasted_iota(jnp.int32, (2 * LANES, LANES), 0)
                 - lax.broadcasted_iota(jnp.int32, (2 * LANES, LANES), 1) - part)
        ahead = ahead & (2 * LANES - 1)
        matrix = jnp.zeros((2 * LANES, LANES), jnp.float32)
        for k, w in enumerate(cubic_weights(jnp.full((8, LANES), lon_fraction[p], jnp.float32))):
            matrix = jnp.where(ahead == k, w[:1, :], matrix)
        high, low = split(matrix)
        lon_weights[p, :, :LANES] = high
        lon_weights[p, :, LANES:] = low
        return carry

    def lon_row(f, p, twice):
        tiles = lon // LANES
        for i in range(tiles):
            tile = full[f][p, :, i * LANES : (i + 1) * LANES]
            twice[i] = tile
            twice[tiles + i] = tile
            if i == 0:
                twice[2 * tiles] = tile
        whole = lax.div(lax.rem(lon_shift[p] - 1 + lon, lon), LANES)
        row = twice[pl.ds(whole, tiles + 2)]
        part = jnp.full((1, 8, LANES), lax.rem(lon_shift[p] - 1 + lon, LANES), jnp.int32)
        near = jnp.where((part >= LANES // 2) & (lane < LANES // 2)[None], row[2:], row[:tiles])
        pairs = jnp.concatenate([near, row[1 : tiles + 1]], axis=2).reshape(8 * tiles, 2 * LANES)
        high, low = split(pairs)
        by_high = jnp.dot(high, lon_weights[p], preferred_element_type=jnp.float32)
        by_low = jnp.dot(low, lon_weights[p, :, :LANES], preferred_element_type=jnp.float32)
        result = by_high[:, :LANES] + (by_high[:, LANES:] + by_low)
        for i in range(tiles):
            tile = result[8 * i : 8 * i + 8]
            moved[p, f, :, i * LANES : (i + 1) * LANES] = tile * scales[f] if f == 2 else tile

    def lon_step(f):
        for c in range(n):
            if chunks[c][0] == f:
                for d in (1, 2, 3):
                    yout(c, d).wait_recv()

        def two_rows(i, carry):
            for j in range(2):
                lon_row(f, 2 * i + j, doubled[j])
            return carry

        lax.fori_loop(0, rows // 2, two_rows, 0)

    lax.fori_loop(0, rows, longitude_matrix, 0)
    for copy in to_smem:
        copy.wait()
    coefficient = lax.fori_loop(0, group, row_weights, jnp.zeros((8, LANES), jnp.float32))
    forward(0)

    def send_sum(step):
        for move in sum_moves(step):
            move.start()

    def add_up(step):
        total = sums[step]
        first = sum(len(peers) for peers in sum_peers[:step])
        for i, move in enumerate(sum_moves(step)):
            move.wait_recv()
            total = total + sums_in[first + i]
        return total

    def wait_sends(c):
        for d in (1, 2, 3):
            yin(c, d).wait_send()
        for k in range(2):
            for d in range(4):
                zmove(c, k, d).wait_send()

    for c in range(n):
        if c + 1 < n:
            forward(c + 1)
        if c == 0:
            for k in range(2):
                table_move(k).wait_recv()
            valid = (sub != 3) & (sub != 7) & (lane < group)
            parts = [jnp.where(valid, table[g], 0.0) for g in range(3)]
            whole = parts[0] + pltpu.roll(parts[1], group, 1) + pltpu.roll(parts[2], 2 * group, 1)
            in_group = (lane >= group) & (lane < 2 * group)
            area = jnp.where(in_group, area_at(first_group_row - group + lane), 0.0)
            sums[0] = whole * jnp.where(sub < 4, area, coefficient)
        if c == X_SUM_TURN:
            sums[2] = add_up(1)
        if c + AHEAD < n:
            start_zown(c + AHEAD)
        if c == 0:
            send_sum(0)
        if c == X_SUM_TURN:
            send_sum(2)
        for f in LON_TURN.get(c, ()):
            lon_step(f)
        if c > 1:
            wait_sends(c - 2)

        piece(c).wait()
        for k in range(2):
            for d in range(4):
                zmove(c, k, d).wait_recv()
        if c == 0:
            sums[1] = add_up(0)

        def interpolate(t, c=c):
            taps = bufs[c][pl.ds(smem_i[0, t], 4)]
            pieces = [taps[:, :, j * LANES : (j + 1) * LANES] for j in range(taps.shape[2] // LANES)]
            return [
                weights[t, 0] * v[0] + weights[t, 1] * v[1] + weights[t, 2] * v[2] + weights[t, 3] * v[3]
                for v in pieces
            ]

        def column(i, carry, c=c):
            t = lax.rem(i + (y + 1) * rows, group)
            for j, value in enumerate(interpolate(t)):
                cols[c][t, :, j * LANES : (j + 1) * LANES] = value
            return carry

        def own_column(p, carry, c=c):
            for j, value in enumerate(interpolate(y * rows + p)):
                first = y * quarter + (chunks[c][1] + j) * LANES
                full[chunks[c][0]][p, :, pl.ds(pl.multiple_of(first, LANES), LANES)] = value
            return carry

        lax.fori_loop(0, group - rows, column, 0, unroll=2)
        if c + 1 < n:
            lax.fori_loop(0, rows, own_column, 0, unroll=2)
        for d in (2, 1, 3):
            yout(c, d).start()
        if c + 1 == n:
            lax.fori_loop(0, rows, own_column, 0, unroll=2)
        if c == 0:
            send_sum(1)

    mass = jnp.sum(add_up(2), axis=1, keepdims=True)
    for f in range(3):
        scales[f] = jnp.broadcast_to(mass[f : f + 1] / mass[f + 4 : f + 5], (8, LANES))

    def scale_row(p, carry):
        for f in range(2):
            for i in range(lon // LANES):
                s = slice(i * LANES, (i + 1) * LANES)
                moved[p, f, :, s] = moved[p, f, :, s] * scales[f]
        return carry

    lax.fori_loop(0, rows, scale_row, 0)
    for c in range(n):
        if c + 2 >= n:
            wait_sends(c)
        else:
            for d in (1, 2, 3):
                yout(c, d).wait_send()
    for d in (1, 2, 3):
        meta(0, d).wait_send()
        meta(1, d).wait_send()
    for k in range(2):
        table_move(k).wait_send()
    for step in range(3):
        for move in sum_moves(step):
            move.wait_send()
    lon_step(2)
    for c in range(n - 2, n):
        for d in (1, 2, 3):
            yout(c, d).wait_send()


def per_device(fields, lat_fraction, lon_fraction, lon_shift, departure_row, extents):
    rows, n_fields, levels, lon = fields.shape
    quarter = lon // NY
    n = len(CHUNKS)
    group = NY * rows
    total_rows = NX * NZ * group
    f32, dma = jnp.float32, pltpu.SemaphoreType.DMA
    widths = [(b - a) * LANES for _, a, b in CHUNKS]
    return pl.pallas_call(
        functools.partial(exchange_kernel, CHUNKS, quarter, total_rows),
        out_shape=pltpu.VMEM(fields.shape, f32),
        in_specs=[pl.BlockSpec(memory_space=pltpu.HBM)] * 6,
        out_specs=pl.BlockSpec(memory_space=pltpu.VMEM),
        scratch_shapes=[pltpu.VMEM((3 * group, levels, w), f32) for w in widths]
        + [pltpu.VMEM((group, levels, w), f32) for w in widths]
        + [pltpu.VMEM((rows, levels, lon), f32)] * n_fields
        + [pltpu.VMEM((2 * lon // LANES + 1, levels, LANES), f32)] * 2
        + [
            pltpu.SMEM((rows,), f32), pltpu.SMEM((rows,), f32), pltpu.SMEM((rows,), jnp.int32),
            pltpu.SMEM((rows,), jnp.int32), pltpu.SMEM((1, 2), jnp.int32), dma((5,)),
            pltpu.VMEM((rows, 2 * LANES, 2 * LANES), jnp.bfloat16),
            pltpu.VMEM((n_fields, 8, LANES), f32),
            pltpu.VMEM(fields.shape, f32),
            pltpu.VMEM((NY + 1, 8, LANES), jnp.int32),
            pltpu.VMEM((NY, 8, LANES), f32),
            pltpu.SMEM((8, LANES), jnp.int32),
            pltpu.SMEM((8, LANES), f32),
            pltpu.VMEM((group, 4, 8, LANES), f32),
            pltpu.VMEM((3, 8, LANES), f32),
            pltpu.VMEM((3, 8, LANES), f32),
            pltpu.VMEM((NX + NZ - 1, 8, LANES), f32),
            dma(()), dma((n,)), dma((n, 3)), dma((n, 3)), dma((n, 2, 4)), dma((n, 2, 4)),
            dma((3,)), dma((3,)), dma((3,)), dma((3,)), dma((2,)), dma((2,)), dma((2,)), dma((NX + NZ - 1,)), dma((NX + NZ - 1,)),
            dma((n, 3)), dma((n, 3)),
        ],
        compiler_params=pltpu.CompilerParams(collective_id=0, has_side_effects=True, vmem_limit_bytes=40 << 20),
    )(*(pltpu.with_memory_space_constraint(a, pltpu.HBM)
        for a in (fields, lat_fraction, lon_fraction, lon_shift, departure_row, extents)))


def solution(mesh):
    finer = Mesh(mesh.devices.reshape(NX, NZ, NY, mesh.shape["lev"]), LAT + ("lev",))
    placed = (P(LAT, None, "lev", None), P(LAT), P(LAT), P(LAT), P(LAT), P(LAT, None))
    return jax.shard_map(
        per_device, mesh=finer, in_specs=placed, out_specs=P(LAT, None, "lev", None), check_vma=False)
```

time: 94.1 us -> 79.4 us (0.84)
  Pallas kernels: 87.4 us -> 77.9 us
  local copies, waits for them, and re-layouts: 6.33 us -> 1.44 us
    pallas_call x1 -> x0, Pallas kernels: 8.44 us -> none  [per_device(): pl.pallas_call(lon_kernel, grid=(rows,), out_shape=jax.ShapeDtypeStruct(f...]
    unnamed x14 -> x1, local copies, waits for them, and re-layouts: 6.33 us -> 1.44 us
    pallas_call x1, Pallas kernels: 79 us -> 77.9 us  [per_device(): pl.pallas_call(functools.partial(exchange_kernel, CHUNKS, quarter, total_...]
where the time goes in v2:
time: 79.4 us; the launch traced here: 79.3 us
  Pallas kernels  77.9 us (98%)
  local copies, waits for them, and re-layouts  1.44 us (2%)
    pallas_call x1, Pallas kernels, per_device(): pl.pallas_call(functools.partial(exchange_kernel, CHUNKS, quarter, total_...  77.9 us

profile of v2, /device:TPU:8, one launch (start us, length us, event | category | flops | bytes accessed | tf_op | source)
XLA Modules:
  0.0 79.3 jit_solution(18168719002477925181)
XLA Ops:
  0.0 77.9 %shard_map.64 = f32[10,3,8,2560]{3,2,1,0:T(8,128)S(1)} custom-call(f32[10,3,8,2560]{3,2,1,0:T(8,128)} %fields.1, f32[10]{0:T(128)} %lat_fraction_in.1, f32[10]{0:T(128)} %lon_fraction_in.1, s32[10]{0:T(128)} %lon_shift_in.1, s32[10]{0:T(128)} %departure_row_in.1, s32[1,2]{1,0:T(1,128)} %extents_in.1), custom_call_target="tpu_custom_call" | custom-call | tf_op jit(solution)/shard_map/pallas_call | solution.py:404
  77.9 1.4 %copy.8 = f32[10,3,8,2560]{3,2,1,0:T(8,128)} copy(f32[10,3,8,2560]{3,2,1,0:T(8,128)S(1)} %shard_map.64) | data formatting | bytes 4915200

commit v3 on v2

--- a/solution.py
+++ b/solution.py
@@ -14,9 +14,10 @@
 NX, NZ, NY = 4, 8, 4
 LANES = 128
 CHUNKS = [(0, 0, 3), (0, 3, 5), (1, 0, 3), (1, 3, 5), (2, 0, 2), (2, 2, 4), (2, 4, 5)]
-LON_TURN = {5: (0, 1)}
-X_SUM_TURN = 3
-AHEAD = 2
+LON_TURN = {4: (0,)}
+Z_SUM_TURN = 3
+AHEAD = 5
+ROWS_AT_ONCE = 5
 
 
 def cubic_weights(t):
@@ -31,7 +32,7 @@
 def split(value):
     scaled = value * 65537.0
     high = scaled - (scaled - value)
-    return high.astype(jnp.bfloat16), (value - high).astype(jnp.bfloat16)
+    return high, value - high
 
 
 def exchange_kernel(
@@ -42,11 +43,11 @@
 ):
     n = len(chunks)
     lon = NY * quarter
-    bufs, cols, full, doubled = scratch[:n], scratch[n : 2 * n], scratch[2 * n : 2 * n + 3], scratch[2 * n + 3 : 2 * n + 5]
+    bufs, cols, full, doubled = scratch[:n], scratch[n : 2 * n], scratch[2 * n : 2 * n + 3], scratch[2 * n + 3 : 2 * n + 3 + ROWS_AT_ONCE]
     (lat_fraction, lon_fraction, lon_shift, departure_row, extents, small_sem, lon_weights, scales,
      own, meta_i, meta_f, smem_i, smem_f, weights, table, sums, sums_in,
      own_sem, piece_sem, yin_send, yin_recv, z_send, z_recv, mi_send, mi_recv, mf_send, mf_recv,
-     smem_sem, tab_send, tab_recv, ar_send, ar_recv, out_send, out_recv) = scratch[2 * n + 5 :]
+     smem_sem, tab_send, tab_recv, ar_send, ar_recv, out_send, out_recv) = scratch[2 * n + 3 + ROWS_AT_ONCE :]
     rows = own.shape[0]
     group = NY * rows
     x, z, y = lax.axis_index("x"), lax.axis_index("z"), lax.axis_index("y")
@@ -61,8 +62,8 @@
 
     sum_peers = [
         [{"lev": 1 - lev}],
+        [{"z": lax.rem(z + d, NZ)} for d in range(1, NZ)],
         [{"x": lax.rem(x + d, NX)} for d in range(1, NX)],
-        [{"z": lax.rem(z + d, NZ)} for d in range(1, NZ)],
     ]
     z_dirs = (1, -1)
 
@@ -79,7 +80,7 @@
     def yin(c, d):
         return pltpu.make_async_remote_copy(
             src_ref=in_fields(c, lax.rem(y + d, NY)), dst_ref=group_rows(c, 1, y),
-            send_sem=yin_send.at[c, d - 1], recv_sem=yin_recv.at[c, d - 1],
+            send_sem=yin_send, recv_sem=yin_recv.at[c, d - 1],
             device_id=y_peer(d), device_id_type=MESH)
 
     def zmove(c, k, d):
@@ -87,11 +88,11 @@
         return pltpu.make_async_remote_copy(
             src_ref=in_fields(c, y) if d == 0 else group_rows(c, 1, source),
             dst_ref=group_rows(c, 0 if k == 0 else 2, source),
-            send_sem=z_send.at[c, k, d], recv_sem=z_recv.at[c, k, d],
+            send_sem=z_send.at[k], recv_sem=z_recv.at[c, k],
             device_id=z_peer(z_dirs[k]), device_id_type=MESH)
 
     def piece(c):
-        return pltpu.make_async_copy(in_fields(c, y), group_rows(c, 1, y), piece_sem.at[c])
+        return pltpu.make_async_copy(in_fields(c, y), group_rows(c, 1, y), piece_sem)
 
     def out_ref(c):
         return full[chunks[c][0]].at[:, :, lanes_of(c, y)]
@@ -99,13 +100,13 @@
     def yout(c, d):
         return pltpu.make_async_remote_copy(
             src_ref=cols[c].at[pl.ds(lax.rem(y + d, NY) * rows, rows)], dst_ref=out_ref(c),
-            send_sem=out_send.at[c, d - 1], recv_sem=out_recv.at[c, d - 1],
+            send_sem=out_send, recv_sem=out_recv.at[c],
             device_id=y_peer(d), device_id_type=MESH)
 
     def meta(which, d):
         ref, s, r = ((meta_i, mi_send, mi_recv), (meta_f, mf_send, mf_recv))[which]
         return pltpu.make_async_remote_copy(
-            src_ref=ref.at[y], dst_ref=ref.at[y], send_sem=s.at[d - 1], recv_sem=r.at[d - 1],
+            src_ref=ref.at[y], dst_ref=ref.at[y], send_sem=s, recv_sem=r,
             device_id=y_peer(d), device_id_type=MESH)
 
     def table_move(k):
@@ -118,10 +119,13 @@
         return [
             pltpu.make_async_remote_copy(
                 src_ref=sums.at[step], dst_ref=sums_in.at[first + i],
-                send_sem=ar_send.at[first + i], recv_sem=ar_recv.at[first + i],
+                send_sem=ar_send.at[step], recv_sem=ar_recv.at[step],
                 device_id=peer, device_id_type=MESH)
             for i, peer in enumerate(sum_peers[step])
         ]
+
+    def wait_bytes(ref, sem):
+        pltpu.make_async_copy(ref, ref, sem).wait()
 
     barrier = pltpu.get_barrier_semaphore()
     partners = [y_peer(d) for d in (1, 2, 3)] + [z_peer(k) for k in z_dirs] + sum(sum_peers, [])
@@ -169,6 +173,20 @@
     mine = (lane >= y * rows) & (lane < (y + 1) * rows)
     facts = jnp.where(mine & (sub == 3), lat_t, jnp.where(mine & (sub == 7), area_lon, 0.0))
 
+    def start_zown(c):
+        for k in range(2):
+            zmove(c, k, 0).start()
+
+    def forward(c):
+        for d in (1, 3, 2):
+            yin(c, d).wait_recv()
+            for k in range(2):
+                zmove(c, k, d).start()
+
+    pl.semaphore_wait(barrier, len(partners))
+    for c in range(AHEAD):
+        start_zown(c)
+
     own_copy.wait()
 
     def row_sums(p, facts):
@@ -182,33 +200,15 @@
         return facts
 
     meta_f[y] = lax.fori_loop(0, rows, row_sums, facts)
-    pl.semaphore_wait(barrier, len(partners))
     for d in (1, 2, 3):
         meta(0, d).start()
         meta(1, d).start()
-
-    def start_yin(c):
+    for c in range(n):
         for d in (2, 1, 3):
             yin(c, d).start()
 
-    def start_zown(c):
-        for k in range(2):
-            zmove(c, k, 0).start()
-
-    def forward(c):
-        for d in (1, 3, 2):
-            yin(c, d).wait_recv()
-            for k in range(2):
-                zmove(c, k, d).start()
-
-    for c in range(n):
-        if c < AHEAD:
-            start_zown(c)
-        start_yin(c)
-
-    for d in (1, 2, 3):
-        meta(0, d).wait_recv()
-        meta(1, d).wait_recv()
+    wait_bytes(meta_i.at[pl.ds(0, NY - 1)], mi_recv)
+    wait_bytes(meta_f.at[pl.ds(0, NY - 1)], mf_recv)
     table[1] = meta_f[0] + meta_f[1] + meta_f[2] + meta_f[3]
     group_starts = meta_i[0] + meta_i[1] + meta_i[2] + meta_i[3]
     meta_i[NY] = group_starts
@@ -236,8 +236,8 @@
         for k, w in enumerate(cubic_weights(jnp.full((8, LANES), lon_fraction[p], jnp.float32))):
             matrix = jnp.where(ahead == k, w[:1, :], matrix)
         high, low = split(matrix)
-        lon_weights[p, :, :LANES] = high
-        lon_weights[p, :, LANES:] = low
+        lon_weights[p, :, :LANES] = high.astype(jnp.bfloat16)
+        lon_weights[p, :, LANES:] = low.astype(jnp.bfloat16)
         return carry
 
     def lon_row(f, p, twice):
@@ -251,28 +251,32 @@
         whole = lax.div(lax.rem(lon_shift[p] - 1 + lon, lon), LANES)
         row = twice[pl.ds(whole, tiles + 2)]
         part = jnp.full((1, 8, LANES), lax.rem(lon_shift[p] - 1 + lon, LANES), jnp.int32)
-        near = jnp.where((part >= LANES // 2) & (lane < LANES // 2)[None], row[2:], row[:tiles])
-        pairs = jnp.concatenate([near, row[1 : tiles + 1]], axis=2).reshape(8 * tiles, 2 * LANES)
-        high, low = split(pairs)
+        wrapped = (part >= LANES // 2) & (lane < LANES // 2)[None]
+
+        def pairs(v):
+            near = jnp.where(wrapped, v[2:], v[:tiles])
+            pair = jnp.concatenate([near, v[1 : tiles + 1]], axis=2).reshape(8 * tiles, 2 * LANES)
+            return pair.astype(jnp.bfloat16)
+
+        high, low = (pairs(v) for v in split(row))
         by_high = jnp.dot(high, lon_weights[p], preferred_element_type=jnp.float32)
         by_low = jnp.dot(low, lon_weights[p, :, :LANES], preferred_element_type=jnp.float32)
         result = by_high[:, :LANES] + (by_high[:, LANES:] + by_low)
         for i in range(tiles):
             tile = result[8 * i : 8 * i + 8]
-            moved[p, f, :, i * LANES : (i + 1) * LANES] = tile * scales[f] if f == 2 else tile
+            moved[p, f, :, i * LANES : (i + 1) * LANES] = tile * scales[f] if f > 0 else tile
 
     def lon_step(f):
         for c in range(n):
             if chunks[c][0] == f:
-                for d in (1, 2, 3):
-                    yout(c, d).wait_recv()
-
-        def two_rows(i, carry):
-            for j in range(2):
-                lon_row(f, 2 * i + j, doubled[j])
+                wait_bytes(cols[c].at[pl.ds(0, group - rows)], out_recv.at[c])
+
+        def some_rows(i, carry):
+            for j in range(ROWS_AT_ONCE):
+                lon_row(f, ROWS_AT_ONCE * i + j, doubled[j])
             return carry
 
-        lax.fori_loop(0, rows // 2, two_rows, 0)
+        lax.fori_loop(0, rows // ROWS_AT_ONCE, some_rows, 0)
 
     lax.fori_loop(0, rows, longitude_matrix, 0)
     for copy in to_smem:
@@ -285,19 +289,13 @@
             move.start()
 
     def add_up(step):
+        count = len(sum_peers[step])
+        first = sum(len(peers) for peers in sum_peers[:step])
+        wait_bytes(sums_in.at[pl.ds(first, count)], ar_recv.at[step])
         total = sums[step]
-        first = sum(len(peers) for peers in sum_peers[:step])
-        for i, move in enumerate(sum_moves(step)):
-            move.wait_recv()
+        for i in range(count):
             total = total + sums_in[first + i]
         return total
-
-    def wait_sends(c):
-        for d in (1, 2, 3):
-            yin(c, d).wait_send()
-        for k in range(2):
-            for d in range(4):
-                zmove(c, k, d).wait_send()
 
     for c in range(n):
         if c + 1 < n:
@@ -311,25 +309,23 @@
             in_group = (lane >= group) & (lane < 2 * group)
             area = jnp.where(in_group, area_at(first_group_row - group + lane), 0.0)
             sums[0] = whole * jnp.where(sub < 4, area, coefficient)
-        if c == X_SUM_TURN:
+        if c == Z_SUM_TURN:
             sums[2] = add_up(1)
         if c + AHEAD < n:
             start_zown(c + AHEAD)
         if c == 0:
             send_sum(0)
-        if c == X_SUM_TURN:
-            send_sum(2)
         for f in LON_TURN.get(c, ()):
             lon_step(f)
-        if c > 1:
-            wait_sends(c - 2)
-
-        piece(c).wait()
+        if c == 0:
+            wait_bytes(fields.at[:, :, :, pl.ds(0, quarter)], piece_sem)
+
         for k in range(2):
-            for d in range(4):
-                zmove(c, k, d).wait_recv()
+            wait_bytes(bufs[c].at[pl.ds(0, group)], z_recv.at[c, k])
         if c == 0:
             sums[1] = add_up(0)
+        if c == Z_SUM_TURN:
+            send_sum(2)
 
         def interpolate(t, c=c):
             taps = bufs[c][pl.ds(smem_i[0, t], 4)]
@@ -356,41 +352,33 @@
             lax.fori_loop(0, rows, own_column, 0, unroll=2)
         for d in (2, 1, 3):
             yout(c, d).start()
+        if c == 0:
+            send_sum(1)
         if c + 1 == n:
             lax.fori_loop(0, rows, own_column, 0, unroll=2)
-        if c == 0:
-            send_sum(1)
 
     mass = jnp.sum(add_up(2), axis=1, keepdims=True)
     for f in range(3):
         scales[f] = jnp.broadcast_to(mass[f : f + 1] / mass[f + 4 : f + 5], (8, LANES))
 
     def scale_row(p, carry):
-        for f in range(2):
-            for i in range(lon // LANES):
-                s = slice(i * LANES, (i + 1) * LANES)
-                moved[p, f, :, s] = moved[p, f, :, s] * scales[f]
+        for i in range(lon // LANES):
+            s = slice(i * LANES, (i + 1) * LANES)
+            moved[p, 0, :, s] = moved[p, 0, :, s] * scales[0]
         return carry
 
     lax.fori_loop(0, rows, scale_row, 0)
-    for c in range(n):
-        if c + 2 >= n:
-            wait_sends(c)
-        else:
-            for d in (1, 2, 3):
-                yout(c, d).wait_send()
-    for d in (1, 2, 3):
-        meta(0, d).wait_send()
-        meta(1, d).wait_send()
+    for step in range(3):
+        wait_bytes(sums_in.at[pl.ds(0, len(sum_peers[step]))], ar_send.at[step])
+    wait_bytes(meta_i.at[pl.ds(0, NY - 1)], mi_send)
+    wait_bytes(meta_f.at[pl.ds(0, NY - 1)], mf_send)
     for k in range(2):
         table_move(k).wait_send()
-    for step in range(3):
-        for move in sum_moves(step):
-            move.wait_send()
+        wait_bytes(fields, z_send.at[k])
+    wait_bytes(fields.at[:, :, :, pl.ds(0, lon - quarter)], yin_send)
+    lon_step(1)
     lon_step(2)
-    for c in range(n - 2, n):
-        for d in (1, 2, 3):
-            yout(c, d).wait_send()
+    wait_bytes(fields.at[:, :, :, pl.ds(0, lon - quarter)], out_send)
 
 
 def per_device(fields, lat_fraction, lon_fraction, lon_shift, departure_row, extents):
@@ -409,7 +397,7 @@
         scratch_shapes=[pltpu.VMEM((3 * group, levels, w), f32) for w in widths]
         + [pltpu.VMEM((group, levels, w), f32) for w in widths]
         + [pltpu.VMEM((rows, levels, lon), f32)] * n_fields
-        + [pltpu.VMEM((2 * lon // LANES + 1, levels, LANES), f32)] * 2
+        + [pltpu.VMEM((2 * lon // LANES + 1, levels, LANES), f32)] * ROWS_AT_ONCE
         + [
             pltpu.SMEM((rows,), f32), pltpu.SMEM((rows,), f32), pltpu.SMEM((rows,), jnp.int32),
             pltpu.SMEM((rows,), jnp.int32), pltpu.SMEM((1, 2), jnp.int32), dma((5,)),
@@ -424,9 +412,9 @@
             pltpu.VMEM((3, 8, LANES), f32),
             pltpu.VMEM((3, 8, LANES), f32),
             pltpu.VMEM((NX + NZ - 1, 8, LANES), f32),
-            dma(()), dma((n,)), dma((n, 3)), dma((n, 3)), dma((n, 2, 4)), dma((n, 2, 4)),
-            dma((3,)), dma((3,)), dma((3,)), dma((3,)), dma((2,)), dma((2,)), dma((2,)), dma((NX + NZ - 1,)), dma((NX + NZ - 1,)),
-            dma((n, 3)), dma((n, 3)),
+            dma(()), dma(()), dma(()), dma((n, 3)), dma((2,)), dma((n, 2)),
+            dma(()), dma(()), dma(()), dma(()), dma((2,)), dma((2,)), dma((2,)), dma((3,)), dma((3,)),
+            dma(()), dma((n,)),
         ],
         compiler_params=pltpu.CompilerParams(collective_id=0, has_side_effects=True, vmem_limit_bytes=40 << 20),
     )(*(pltpu.with_memory_space_constraint(a, pltpu.HBM)

time: 79.4 us -> 72.7 us (0.916)
  Pallas kernels: 77.9 us -> 71 us
    pallas_call x1, Pallas kernels: 77.9 us -> 71 us  [per_device(): pl.pallas_call(functools.partial(exchange_kernel, CHUNKS, quarter, total_...]
where the time goes in v3:
time: 72.7 us; the launch traced here: 72.5 us
  Pallas kernels  71 us (98%)
  local copies, waits for them, and re-layouts  1.44 us (2%)
    pallas_call x1, Pallas kernels, per_device(): pl.pallas_call(functools.partial(exchange_kernel, CHUNKS, quarter, total_...  71 us

profile of v3, /device:TPU:8, one launch (start us, length us, event | category | flops | bytes accessed | tf_op | source)
XLA Modules:
  0.0 72.5 jit_solution(6445447050089585840)
XLA Ops:
  0.0 71.0 %shard_map.64 = f32[10,3,8,2560]{3,2,1,0:T(8,128)S(1)} custom-call(f32[10,3,8,2560]{3,2,1,0:T(8,128)} %fields.1, f32[10]{0:T(128)} %lat_fraction_in.1, f32[10]{0:T(128)} %lon_fraction_in.1, s32[10]{0:T(128)} %lon_shift_in.1, s32[10]{0:T(128)} %departure_row_in.1, s32[1,2]{1,0:T(1,128)} %extents_in.1), custom_call_target="tpu_custom_call" | custom-call | tf_op jit(solution)/shard_map/pallas_call | solution.py:392
  71.0 1.4 %copy.8 = f32[10,3,8,2560]{3,2,1,0:T(8,128)} copy(f32[10,3,8,2560]{3,2,1,0:T(8,128)S(1)} %shard_map.64) | data formatting | bytes 4915200

commit v4 on v3

--- a/solution.py
+++ b/solution.py
@@ -13,10 +13,11 @@
 LAT = ("x", "z", "y")
 NX, NZ, NY = 4, 8, 4
 LANES = 128
-CHUNKS = [(0, 0, 3), (0, 3, 5), (1, 0, 3), (1, 3, 5), (2, 0, 2), (2, 2, 4), (2, 4, 5)]
+CHUNKS = [(0, 0, 3), (0, 3, 5), (1, 0, 3), (1, 3, 5), (2, 0, 2), (2, 2, 3), (2, 3, 4), (2, 4, 5)]
 LON_TURN = {4: (0,)}
 Z_SUM_TURN = 3
 AHEAD = 5
+DEEP_FROM = 4
 ROWS_AT_ONCE = 5
 
 
@@ -173,6 +174,10 @@
     mine = (lane >= y * rows) & (lane < (y + 1) * rows)
     facts = jnp.where(mine & (sub == 3), lat_t, jnp.where(mine & (sub == 7), area_lon, 0.0))
 
+    def start_yin(c):
+        for d in (2, 1, 3):
+            yin(c, d).start()
+
     def start_zown(c):
         for k in range(2):
             zmove(c, k, 0).start()
@@ -184,7 +189,9 @@
                 zmove(c, k, d).start()
 
     pl.semaphore_wait(barrier, len(partners))
-    for c in range(AHEAD):
+    start_zown(0)
+    start_yin(0)
+    for c in range(1, AHEAD):
         start_zown(c)
 
     own_copy.wait()
@@ -203,9 +210,8 @@
     for d in (1, 2, 3):
         meta(0, d).start()
         meta(1, d).start()
-    for c in range(n):
-        for d in (2, 1, 3):
-            yin(c, d).start()
+    for c in range(1, n):
+        start_yin(c)
 
     wait_bytes(meta_i.at[pl.ds(0, NY - 1)], mi_recv)
     wait_bytes(meta_f.at[pl.ds(0, NY - 1)], mf_recv)
@@ -298,8 +304,9 @@
         return total
 
     for c in range(n):
-        if c + 1 < n:
-            forward(c + 1)
+        for later in range(n):
+            if later == c + 1 + (c >= DEEP_FROM) or (c == DEEP_FROM and later == c + 1):
+                forward(later)
         if c == 0:
             for k in range(2):
                 table_move(k).wait_recv()

time: 72.7 us -> 72.1 us (level)
    pallas_call x1, Pallas kernels: 71 us -> 70.3 us  [per_device(): pl.pallas_call(functools.partial(exchange_kernel, CHUNKS, quarter, total_...]
where the time goes in v4:
time: 72.1 us; the launch traced here: 71.7 us
  Pallas kernels  70.3 us (98%)
  local copies, waits for them, and re-layouts  1.44 us (2%)
    pallas_call x1, Pallas kernels, per_device(): pl.pallas_call(functools.partial(exchange_kernel, CHUNKS, quarter, total_...  70.3 us

profile of v4, /device:TPU:8, one launch (start us, length us, event | category | flops | bytes accessed | tf_op | source)
XLA Modules:
  0.0 71.7 jit_solution(10313632807672170361)
XLA Ops:
  0.0 70.3 %shard_map.64 = f32[10,3,8,2560]{3,2,1,0:T(8,128)S(1)} custom-call(f32[10,3,8,2560]{3,2,1,0:T(8,128)} %fields.1, f32[10]{0:T(128)} %lat_fraction_in.1, f32[10]{0:T(128)} %lon_fraction_in.1, s32[10]{0:T(128)} %lon_shift_in.1, s32[10]{0:T(128)} %departure_row_in.1, s32[1,2]{1,0:T(1,128)} %extents_in.1), custom_call_target="tpu_custom_call" | custom-call | tf_op jit(solution)/shard_map/pallas_call | solution.py:399
  70.3 1.4 %copy.8 = f32[10,3,8,2560]{3,2,1,0:T(8,128)} copy(f32[10,3,8,2560]{3,2,1,0:T(8,128)S(1)} %shard_map.64) | data formatting | bytes 4915200

commit v5 on v4

--- a/solution.py
+++ b/solution.py
@@ -36,19 +36,46 @@
     return high, value - high
 
 
+def lon_row(source, p, twice, lon_shift, lon_weights):
+    lon = source.shape[-1]
+    tiles = lon // LANES
+    lane = lax.broadcasted_iota(jnp.int32, (8, LANES), 1)
+    for i in range(tiles):
+        tile = source[p, :, i * LANES : (i + 1) * LANES]
+        twice[i] = tile
+        twice[tiles + i] = tile
+        if i == 0:
+            twice[2 * tiles] = tile
+    whole = lax.div(lax.rem(lon_shift[p] - 1 + lon, lon), LANES)
+    row = twice[pl.ds(whole, tiles + 2)]
+    part = jnp.full((1, 8, LANES), lax.rem(lon_shift[p] - 1 + lon, LANES), jnp.int32)
+    wrapped = (part >= LANES // 2) & (lane < LANES // 2)[None]
+
+    def pairs(v):
+        near = jnp.where(wrapped, v[2:], v[:tiles])
+        pair = jnp.concatenate([near, v[1 : tiles + 1]], axis=2).reshape(8 * tiles, 2 * LANES)
+        return pair.astype(jnp.bfloat16)
+
+    high, low = (pairs(v) for v in split(row))
+    by_high = jnp.dot(high, lon_weights[p], preferred_element_type=jnp.float32)
+    by_low = jnp.dot(low, lon_weights[p, :, :LANES], preferred_element_type=jnp.float32)
+    result = by_high[:, :LANES] + (by_high[:, LANES:] + by_low)
+    return [result[8 * i : 8 * i + 8] for i in range(tiles)]
+
+
 def exchange_kernel(
     chunks, quarter, total_rows,
     fields, lat_fraction_in, lon_fraction_in, lon_shift_in, departure_row_in, extents_in,
-    moved,
+    moved, last_full, lon_weights, scales, shifts,
     *scratch,
 ):
     n = len(chunks)
     lon = NY * quarter
-    bufs, cols, full, doubled = scratch[:n], scratch[n : 2 * n], scratch[2 * n : 2 * n + 3], scratch[2 * n + 3 : 2 * n + 3 + ROWS_AT_ONCE]
-    (lat_fraction, lon_fraction, lon_shift, departure_row, extents, small_sem, lon_weights, scales,
+    bufs, cols, full, doubled = scratch[:n], scratch[n : 2 * n], (*scratch[2 * n : 2 * n + 2], last_full), scratch[2 * n + 2 : 2 * n + 2 + ROWS_AT_ONCE]
+    (lat_fraction, lon_fraction, lon_shift, departure_row, extents, small_sem,
      own, meta_i, meta_f, smem_i, smem_f, weights, table, sums, sums_in,
      own_sem, piece_sem, yin_send, yin_recv, z_send, z_recv, mi_send, mi_recv, mf_send, mf_recv,
-     smem_sem, tab_send, tab_recv, ar_send, ar_recv, out_send, out_recv) = scratch[2 * n + 3 + ROWS_AT_ONCE :]
+     smem_sem, tab_send, tab_recv, ar_send, ar_recv, out_send, out_recv) = scratch[2 * n + 2 + ROWS_AT_ONCE :]
     rows = own.shape[0]
     group = NY * rows
     x, z, y = lax.axis_index("x"), lax.axis_index("z"), lax.axis_index("y")
@@ -81,7 +108,7 @@
     def yin(c, d):
         return pltpu.make_async_remote_copy(
             src_ref=in_fields(c, lax.rem(y + d, NY)), dst_ref=group_rows(c, 1, y),
-            send_sem=yin_send, recv_sem=yin_recv.at[c, d - 1],
+            send_sem=yin_send, recv_sem=yin_recv.at[c],
             device_id=y_peer(d), device_id_type=MESH)
 
     def zmove(c, k, d):
@@ -89,7 +116,7 @@
         return pltpu.make_async_remote_copy(
             src_ref=in_fields(c, y) if d == 0 else group_rows(c, 1, source),
             dst_ref=group_rows(c, 0 if k == 0 else 2, source),
-            send_sem=z_send.at[k], recv_sem=z_recv.at[c, k],
+            send_sem=z_send.at[k], recv_sem=z_recv.at[c],
             device_id=z_peer(z_dirs[k]), device_id_type=MESH)
 
     def piece(c):
@@ -183,8 +210,8 @@
             zmove(c, k, 0).start()
 
     def forward(c):
+        wait_bytes(bufs[c].at[pl.ds(0, group - rows)], yin_recv.at[c])
         for d in (1, 3, 2):
-            yin(c, d).wait_recv()
             for k in range(2):
                 zmove(c, k, d).start()
 
@@ -246,32 +273,6 @@
         lon_weights[p, :, LANES:] = low.astype(jnp.bfloat16)
         return carry
 
-    def lon_row(f, p, twice):
-        tiles = lon // LANES
-        for i in range(tiles):
-            tile = full[f][p, :, i * LANES : (i + 1) * LANES]
-            twice[i] = tile
-            twice[tiles + i] = tile
-            if i == 0:
-                twice[2 * tiles] = tile
-        whole = lax.div(lax.rem(lon_shift[p] - 1 + lon, lon), LANES)
-        row = twice[pl.ds(whole, tiles + 2)]
-        part = jnp.full((1, 8, LANES), lax.rem(lon_shift[p] - 1 + lon, LANES), jnp.int32)
-        wrapped = (part >= LANES // 2) & (lane < LANES // 2)[None]
-
-        def pairs(v):
-            near = jnp.where(wrapped, v[2:], v[:tiles])
-            pair = jnp.concatenate([near, v[1 : tiles + 1]], axis=2).reshape(8 * tiles, 2 * LANES)
-            return pair.astype(jnp.bfloat16)
-
-        high, low = (pairs(v) for v in split(row))
-        by_high = jnp.dot(high, lon_weights[p], preferred_element_type=jnp.float32)
-        by_low = jnp.dot(low, lon_weights[p, :, :LANES], preferred_element_type=jnp.float32)
-        result = by_high[:, :LANES] + (by_high[:, LANES:] + by_low)
-        for i in range(tiles):
-            tile = result[8 * i : 8 * i + 8]
-            moved[p, f, :, i * LANES : (i + 1) * LANES] = tile * scales[f] if f > 0 else tile
-
     def lon_step(f):
         for c in range(n):
             if chunks[c][0] == f:
@@ -279,7 +280,9 @@
 
         def some_rows(i, carry):
             for j in range(ROWS_AT_ONCE):
-                lon_row(f, ROWS_AT_ONCE * i + j, doubled[j])
+                p = ROWS_AT_ONCE * i + j
+                for k, tile in enumerate(lon_row(full[f], p, doubled[j], lon_shift, lon_weights)):
+                    moved[p, f, :, k * LANES : (k + 1) * LANES] = tile * scales[f] if f > 0 else tile
             return carry
 
         lax.fori_loop(0, rows // ROWS_AT_ONCE, some_rows, 0)
@@ -327,8 +330,7 @@
         if c == 0:
             wait_bytes(fields.at[:, :, :, pl.ds(0, quarter)], piece_sem)
 
-        for k in range(2):
-            wait_bytes(bufs[c].at[pl.ds(0, group)], z_recv.at[c, k])
+        wait_bytes(bufs[c].at[pl.ds(0, 2 * group)], z_recv.at[c])
         if c == 0:
             sums[1] = add_up(0)
         if c == Z_SUM_TURN:
@@ -384,8 +386,28 @@
         wait_bytes(fields, z_send.at[k])
     wait_bytes(fields.at[:, :, :, pl.ds(0, lon - quarter)], yin_send)
     lon_step(1)
-    lon_step(2)
+    for p in range(rows):
+        shifts[p] = lon_shift[p]
+    for c in range(n):
+        if chunks[c][0] == 2:
+            wait_bytes(cols[c].at[pl.ds(0, group - rows)], out_recv.at[c])
     wait_bytes(fields.at[:, :, :, pl.ds(0, lon - quarter)], out_send)
+
+
+def finish_kernel(moved, last_full, lon_weights, scales, shifts, out, *scratch):
+    staged, doubled, sems = scratch[0], scratch[1:-1], scratch[-1]
+    rows = last_full.shape[0]
+    copies = [pltpu.make_async_copy(moved, out.at[:, pl.ds(0, 2)], sems.at[0])]
+    copies[0].start()
+    for first in range(0, rows, ROWS_AT_ONCE):
+        for j in range(ROWS_AT_ONCE):
+            for k, tile in enumerate(lon_row(last_full, first + j, doubled[j], shifts, lon_weights)):
+                staged[first + j, :, k * LANES : (k + 1) * LANES] = tile * scales[2]
+        part = pl.ds(first, ROWS_AT_ONCE)
+        copies.append(pltpu.make_async_copy(staged.at[part], out.at[part, 2], sems.at[len(copies)]))
+        copies[-1].start()
+    for copy in copies:
+        copy.wait()
 
 
 def per_device(fields, lat_fraction, lon_fraction, lon_shift, departure_row, extents):
@@ -395,21 +417,24 @@
     group = NY * rows
     total_rows = NX * NZ * group
     f32, dma = jnp.float32, pltpu.SemaphoreType.DMA
+    twice = [pltpu.VMEM((2 * lon // LANES + 1, levels, LANES), f32)] * ROWS_AT_ONCE
+    kept = (*[pl.BlockSpec(memory_space=pltpu.VMEM)] * 4, pl.BlockSpec(memory_space=pltpu.SMEM))
     widths = [(b - a) * LANES for _, a, b in CHUNKS]
-    return pl.pallas_call(
+    parts = pl.pallas_call(
         functools.partial(exchange_kernel, CHUNKS, quarter, total_rows),
-        out_shape=pltpu.VMEM(fields.shape, f32),
+        out_shape=(
+            pltpu.VMEM((rows, n_fields - 1, levels, lon), f32), pltpu.VMEM((rows, levels, lon), f32),
+            pltpu.VMEM((rows, 2 * LANES, 2 * LANES), jnp.bfloat16), pltpu.VMEM((n_fields, 8, LANES), f32),
+            pltpu.SMEM((rows,), jnp.int32)),
         in_specs=[pl.BlockSpec(memory_space=pltpu.HBM)] * 6,
-        out_specs=pl.BlockSpec(memory_space=pltpu.VMEM),
+        out_specs=kept,
         scratch_shapes=[pltpu.VMEM((3 * group, levels, w), f32) for w in widths]
         + [pltpu.VMEM((group, levels, w), f32) for w in widths]
-        + [pltpu.VMEM((rows, levels, lon), f32)] * n_fields
-        + [pltpu.VMEM((2 * lon // LANES + 1, levels, LANES), f32)] * ROWS_AT_ONCE
+        + [pltpu.VMEM((rows, levels, lon), f32)] * (n_fields - 1)
+        + twice
         + [
             pltpu.SMEM((rows,), f32), pltpu.SMEM((rows,), f32), pltpu.SMEM((rows,), jnp.int32),
             pltpu.SMEM((rows,), jnp.int32), pltpu.SMEM((1, 2), jnp.int32), dma((5,)),
-            pltpu.VMEM((rows, 2 * LANES, 2 * LANES), jnp.bfloat16),
-            pltpu.VMEM((n_fields, 8, LANES), f32),
             pltpu.VMEM(fields.shape, f32),
             pltpu.VMEM((NY + 1, 8, LANES), jnp.int32),
             pltpu.VMEM((NY, 8, LANES), f32),
@@ -419,13 +444,21 @@
             pltpu.VMEM((3, 8, LANES), f32),
             pltpu.VMEM((3, 8, LANES), f32),
             pltpu.VMEM((NX + NZ - 1, 8, LANES), f32),
-            dma(()), dma(()), dma(()), dma((n, 3)), dma((2,)), dma((n, 2)),
+            dma(()), dma(()), dma(()), dma((n,)), dma((2,)), dma((n,)),
             dma(()), dma(()), dma(()), dma(()), dma((2,)), dma((2,)), dma((2,)), dma((3,)), dma((3,)),
             dma(()), dma((n,)),
         ],
         compiler_params=pltpu.CompilerParams(collective_id=0, has_side_effects=True, vmem_limit_bytes=40 << 20),
     )(*(pltpu.with_memory_space_constraint(a, pltpu.HBM)
         for a in (fields, lat_fraction, lon_fraction, lon_shift, departure_row, extents)))
+    return pl.pallas_call(
+        finish_kernel,
+        out_shape=jax.ShapeDtypeStruct(fields.shape, f32),
+        in_specs=list(kept),
+        out_specs=pl.BlockSpec(memory_space=pltpu.HBM),
+        scratch_shapes=[pltpu.VMEM((rows, levels, lon), f32)] + twice + [pltpu.SemaphoreType.DMA((1 + rows // ROWS_AT_ONCE,))],
+        compiler_params=pltpu.CompilerParams(vmem_limit_bytes=16 << 20),
+    )(*parts)
 
 
 def solution(mesh):

time: 72.1 us -> 71.5 us (level)
  local copies, waits for them, and re-layouts: 1.44 us -> 0 us
    pallas_call x0 -> x1, Pallas kernels: none -> 1.82 us  [per_device(): pl.pallas_call(finish_kernel, out_shape=jax.ShapeDtypeStruct(fields.shape...]
    unnamed x1 -> x0, local copies, waits for them, and re-layouts: 1.44 us -> none
    pallas_call x1, Pallas kernels: 70.3 us -> 69.2 us  [per_device(): pl.pallas_call(functools.partial(exchange_kernel, CHUNKS, quarter, total_...]
where the time goes in v5:
time: 71.5 us; the launch traced here: 71 us
  Pallas kernels  71 us (99%)
    pallas_call x1, Pallas kernels, per_device(): pl.pallas_call(functools.partial(exchange_kernel, CHUNKS, quarter, total_...  69.2 us
    pallas_call x1, Pallas kernels, per_device(): pl.pallas_call(finish_kernel, out_shape=jax.ShapeDtypeStruct(fields.shape...  1.82 us

profile of v5, /device:TPU:8, one launch (start us, length us, event | category | flops | bytes accessed | tf_op | source)
XLA Modules:
  0.0 71.0 jit_solution(7980633486292859308)
XLA Ops:
  0.0 69.2 %shard_map.64 = (f32[10,2,8,2560]{3,2,1,0:T(8,128)S(1)}, f32[10,8,2560]{2,1,0:T(8,128)S(1)}, bf16[10,256,256]{2,1,0:T(8,128)(2,1)S(1)}, f32[3,8,128]{2,1,0:T(8,128)S(1)}, s32[10]{0:T(128)S(4)}) custom-call(f32[10,3,8,2560]{3,2,1,0:T(8,128)} %fields.1, f32[10]{0:T(128)} %lat_fraction_in.1, f32[10]{0:T(128)} %lon_fraction_in.1, s32[10]{0:T(128)} %lon_shift_in.1, ...), custom_call_target="tpu_custom_call" | custom-call | tf_op jit(solution)/shard_map/pallas_call | solution.py:423
  69.2 1.8 %shard_map.65 = f32[10,3,8,2560]{3,2,1,0:T(8,128)} custom-call(f32[10,2,8,2560]{3,2,1,0:T(8,128)S(1)} %get-tuple-element.10.moved, f32[10,8,2560]{2,1,0:T(8,128)S(1)} %get-tuple-element.11.last_full, bf16[10,256,256]{2,1,0:T(8,128)(2,1)S(1)} %get-tuple-element.12.lon_weights, f32[3,8,128]{2,1,0:T(8,128)S(1)} %get-tuple-element.13.scales, ...), custom_call_target="tpu_custom_call" | custom-call | tf_op jit(solution)/shard_map/pallas_call | solution.py:454
